TPU v7x, 32 devices: a whole 2x2x4 slice. The times are simulated.
32 devices in a mesh: date: 16 (over z, y, x), pix: 2 (over core).
Axes of the slice: x: 2, y: 2, z: 4, core: 2. Of those that a mesh axis runs over, the one named last changes fastest.
Arguments:
- reflect: bfloat16 [64, 6, 16384], P('date', None, 'pix'), may hold values from -8 to 8
- cloud_free: int32 [64, 16384], P('date', 'pix'), may hold values from 0 to 1, as said below
- days: int32 [64], P('date'), may hold values from 1 to 2079, as said below
Outputs:
- median: float32 [6, 16384], P(None, 'pix')
- slope: float32 [6, 16384], P(None, 'pix')
Inputs may be any that keep to these rules, and one draw needn't show every extreme that they name: `cloud_free`: every pixel is clear on at least one of the first 32 dates and on at least one of the others; clear shares differ between tiles. `days`: strictly increasing.
All inputs are finite; a program needn't handle non-finite values.
Results may differ from a plain program's by a relative error of at most 0.0003.
Values may be sent and summed in bfloat16 or wider, within the bound.
No kernel may reach another device: no remote copies, remote signals or barrier semaphores. Data moves between devices by JAX's collectives and lax.ppermute only.
A program may use at most 64 MiB of HBM per device.

v0:
```python
import jax
import jax.numpy as jnp
from jax import lax
from jax.sharding import PartitionSpec as P

ridge = 1.0
sentinel = 100.0


def count_ranks(carry, own, piece):

    def step(i, state):
        less, equal, count = state
        other = lax.dynamic_index_in_dim(piece, i, 0, keepdims=True).astype(jnp.float32)
        less = less + (other < own).astype(jnp.float32)
        equal = equal + (other == own).astype(jnp.float32)
        count = count + (other[0, 0] < 50.0).astype(jnp.float32)
        return (less, equal, count)

    return lax.fori_loop(0, piece.shape[0], step, carry)


def select_sums(values, valid, less, equal, count):
    lower = jnp.floor((count - 1.0) / 2.0)
    upper = jnp.floor(count / 2.0)
    low_pick = valid[:, None, :] * ((less <= lower) & (lower < less + equal)).astype(jnp.float32)
    high_pick = valid[:, None, :] * ((less <= upper) & (upper < less + equal)).astype(jnp.float32)
    return (
        jnp.sum(low_pick * values, 0),
        jnp.sum(low_pick, 0),
        jnp.sum(high_pick * values, 0),
        jnp.sum(high_pick, 0),
    )


def finish_median(low_num, low_den, high_num, high_den):
    return 0.5 * (low_num / jnp.maximum(low_den, 1.0) + high_num / jnp.maximum(high_den, 1.0))


def column_median(moved):
    column = moved.astype(jnp.float32)
    column_valid = (column[:, 0, :] < 50.0).astype(jnp.float32)
    zeros = jnp.zeros(column.shape, jnp.float32)
    start_carry = (zeros, zeros, jnp.zeros((column.shape[2],), jnp.float32))
    less, equal, count = count_ranks(start_carry, column, moved)
    low_num, low_den, high_num, high_den = select_sums(column, column_valid, less, equal, count)
    return (column, column_valid, finish_median(low_num, low_den, high_num, high_den))


def fit_slope(s_zero, s_one, s_two, s_y, s_ty):
    first = s_zero + ridge
    determinant = first * (s_two + ridge) - s_one * s_one
    return (first[None, :] * s_ty - s_one[None, :] * s_y) / determinant[None, :]


def local(reflect, cloud_free, days):
    values = reflect.astype(jnp.float32)
    valid = cloud_free.astype(jnp.float32)
    years = days.astype(jnp.float32) / 365.0
    csum = jnp.sum(values * valid[:, None, :], 2)
    cnt = jnp.sum(valid, 1)
    csum, cnt = lax.psum((csum, cnt), "pix")
    scene_mean = csum / jnp.maximum(cnt, 1.0)[:, None]
    marked = jnp.where(valid[:, None, :] > 0, values, sentinel).astype(jnp.bfloat16)
    shifted = values - scene_mean[:, :, None]
    weighted = valid[:, None, :] * shifted
    s_zero = jnp.sum(valid, 0)
    s_one = jnp.sum(years[:, None] * valid, 0)
    s_two = jnp.sum((years * years)[:, None] * valid, 0)
    s_y = jnp.sum(weighted, 0)
    s_ty = jnp.sum(years[:, None, None] * weighted, 0)
    moved = lax.all_to_all(marked, "date", split_axis=2, concat_axis=0, tiled=True)
    column, column_valid, part_median = column_median(moved)
    median = lax.all_gather(part_median, "date", axis=1, tiled=True)
    s_y, s_ty, s_zero, s_one, s_two = lax.psum((s_y, s_ty, s_zero, s_one, s_two), "date")
    slope = fit_slope(s_zero, s_one, s_two, s_y, s_ty)
    return (median, slope)


def solution(mesh):
    placed = (P("date", None, "pix"), P("date", "pix"), P("date"))
    return jax.shard_map(
        local,
        mesh=mesh,
        in_specs=placed,
        out_specs=(P(None, "pix"), P(None, "pix")),
        check_vma=False,
    )
```

profile of v0, /device:TPU:0, one launch (start us, length us, event | category | flops | bytes accessed | tf_op | source)
XLA Modules:
  0.0 414.7 jit_solution(17819752993265104546)
XLA Ops:
  7.9 1.8 convert_reduce_fusion.1
  9.7 0.9 convert_element_type.50
  10.7 1.0 broadcast_compare_fusion
  11.6 1.3 fusion.4
  12.9 2.6 all-reduce.2
  15.6 3.0 fusion.8
  18.6 8.5 %copy.37 = bf16[4,6,8192]{1,0,2:T(4,128)(2,1)} copy(bf16[4,6,8192]{2,0,1:T(4,128)(2,1)S(1)} %get-tuple-element.172) | data formatting | bytes 786432 | tf_op jit(solution)/shard_map/convert_element_type | solution.py:64
  27.2 14.3 %reshape.24 = bf16[16,2,6144]{2,1,0:T(2,128)(2,1)} reshape(bf16[8192,4,6]{2,1,0:T(4,128)(2,1)} %bitcast.17) | data formatting | bytes 786432
  41.5 8.2 %all-to-all-start = ((bf16[16,2,6144]{2,1,0:T(2,128)(2,1)}), bf16[16,2,6144]{2,1,0:T(2,128)(2,1)S(1)}, u32[]{:S(2)}, u32[]{:S(2)}) async-start(bf16[16,2,6144]{2,1,0:T(2,128)(2,1)} %reshape.24), calls=%async_computation | async-start | bytes 786432 | tf_op jit(solution)/shard_map/all_to_all | solution.py:72
  49.7 72.8 %all-reduce.6.cloned.1.call-done = (f32[8192]{0:T(1024)}, f32[8192]{0:T(1024)}, f32[8192]{0:T(1024)}) async-done(((f32[8192]{0:T(1024)}, f32[8192]{0:T(1024)}, f32[8192]{0:T(1024)}), (f32[8192]{0:T(1024)}, f32[8192]{0:T(1024)}, f32[8192]{0:T(1024)})) %all-reduce.6.cloned.1.call-update) | async-done | bytes 98320 | tf_op jit(solution)/shard_map/psum | solution.py:75
  122.5 0.8 broadcast_add_fusion
  123.4 114.3 %all-reduce.8.cloned.1.call-done = (f32[6,8192]{1,0:T(8,128)}, f32[6,8192]{1,0:T(8,128)}) async-done(((f32[6,8192]{1,0:T(8,128)}, f32[6,8192]{1,0:T(8,128)}), (f32[6,8192]{1,0:T(8,128)}, f32[6,8192]{1,0:T(8,128)})) %all-reduce.8.cloned.1.call-update) | async-done | bytes 393232 | tf_op jit(solution)/shard_map/psum | solution.py:75
  237.7 1.8 subtract_divide_fusion
  239.5 20.0 %reshape.25 = bf16[8192,4,6]{2,1,0:T(4,128)(2,1)} reshape(bf16[16,2,6144]{2,1,0:T(2,128)(2,1)S(1)} %all-to-all-done) | data formatting | bytes 786432
  259.5 12.9 %copy.38 = bf16[16,4,6,512]{3,2,1,0:T(8,128)(2,1)} copy(bf16[16,4,6,512]{2,1,3,0:T(4,128)(2,1)} %bitcast.18) | data formatting | bytes 786432 | tf_op jit(solution)/shard_map/all_to_all | solution.py:72
  272.3 1.2 bitcast_convert_fusion
  273.7 91.0 %while.18 = (s32[]{:T(128)}, f32[64,6,512]{2,1,0:T(8,128)S(1)}, f32[64,6,512]{2,1,0:T(8,128)S(1)}, f32[512]{0:T(512)S(1)}, bf16[64,6,512]{2,1,0:T(8,128)(2,1)}, ...) while((s32[]{:T(128)}, f32[64,6,512]{2,1,0:T(8,128)S(1)}, f32[64,6,512]{2,1,0:T(8,128)S(1)}, ...), condition=%wide.region_1.0_spmd.clone, body=%wide.region_0.0_spmd.clone.sunk | while | flops 1577987 | bytes 3985508 | solution.py:20
  273.7 0.7 dynamic-slice_convert_fusion.2
  275.1 0.7 dynamic-slice_convert_fusion.2
  276.5 0.7 dynamic-slice_convert_fusion.2
  277.9 0.7 dynamic-slice_convert_fusion.2
  279.4 0.7 dynamic-slice_convert_fusion.2
  280.8 0.7 dynamic-slice_convert_fusion.2
  282.2 0.7 dynamic-slice_convert_fusion.2
  283.6 0.7 dynamic-slice_convert_fusion.2
  285.1 0.7 dynamic-slice_convert_fusion.2
  286.5 0.7 dynamic-slice_convert_fusion.2
  292.2 0.7 dynamic-slice_convert_fusion.2
  293.6 0.7 dynamic-slice_convert_fusion.2
  295.0 0.7 dynamic-slice_convert_fusion.2
  296.4 0.7 dynamic-slice_convert_fusion.2
  297.9 0.7 dynamic-slice_convert_fusion.2
  299.3 0.7 dynamic-slice_convert_fusion.2
  300.7 0.7 dynamic-slice_convert_fusion.2
  302.1 0.7 dynamic-slice_convert_fusion.2
  303.5 0.7 dynamic-slice_convert_fusion.2
  305.0 0.7 dynamic-slice_convert_fusion.2
  306.4 0.7 dynamic-slice_convert_fusion.2
  307.8 0.7 dynamic-slice_convert_fusion.2
  309.2 0.7 dynamic-slice_convert_fusion.2
  310.6 0.7 dynamic-slice_convert_fusion.2
  312.1 0.7 dynamic-slice_convert_fusion.2
  313.5 0.7 dynamic-slice_convert_fusion.2
  319.2 0.7 dynamic-slice_convert_fusion.2
  320.6 0.7 dynamic-slice_convert_fusion.2
  322.0 0.7 dynamic-slice_convert_fusion.2
  323.4 0.7 dynamic-slice_convert_fusion.2
  324.9 0.7 dynamic-slice_convert_fusion.2
  326.3 0.7 dynamic-slice_convert_fusion.2
  327.7 0.7 dynamic-slice_convert_fusion.2
  329.1 0.7 dynamic-slice_convert_fusion.2
  330.5 0.7 dynamic-slice_convert_fusion.2
  332.0 0.7 dynamic-slice_convert_fusion.2
  333.4 0.7 dynamic-slice_convert_fusion.2
  334.8 0.7 dynamic-slice_convert_fusion.2
  336.2 0.7 dynamic-slice_convert_fusion.2
  337.7 0.7 dynamic-slice_convert_fusion.2
  339.1 0.7 dynamic-slice_convert_fusion.2
  340.5 0.7 dynamic-slice_convert_fusion.2
  346.2 0.7 dynamic-slice_convert_fusion.2
  347.6 0.7 dynamic-slice_convert_fusion.2
  349.0 0.7 dynamic-slice_convert_fusion.2
  365.1 1.6 fusion.1
  366.8 40.4 %all_gather.3 = f32[6,8192]{1,0:T(8,128)S(1)} all-gather(f32[6,512]{1,0:T(8,128)S(1)} %add_multiply_fusion), channel_id=1, replica_groups=mesh['date'=16,'pix'=2] {'date'}, dimensions={1}, use_global_device_ids=true | all-gather | bytes 208896 | tf_op jit(solution)/shard_map/all_gather | solution.py:74
  (228 shorter events, 59.5 us)
Async XLA Ops:
  7.2 115.4 %all-reduce.6.cloned.1.call-start = ((), (), s32[]{:S(2)}) async-start(), calls=%async_computation.1 | async-start | bytes 196608 | tf_op jit(solution)/shard_map/psum | solution.py:75
  9.7 228.0 %all-reduce.8.cloned.1.call-start = ((), (), s32[]{:S(2)}) async-start(), calls=%async_computation.2 | async-start | bytes 1048576 | tf_op jit(solution)/shard_map/psum | solution.py:75
  41.5 198.0 %all-to-all-start = ((bf16[16,2,6144]{2,1,0:T(2,128)(2,1)}), bf16[16,2,6144]{2,1,0:T(2,128)(2,1)S(1)}, u32[]{:S(2)}, u32[]{:S(2)}) async-start(bf16[16,2,6144]{2,1,0:T(2,128)(2,1)} %reshape.24), calls=%async_computation | async-start | bytes 786432 | tf_op jit(solution)/shard_map/all_to_all | solution.py:72
Sparse Core Ops, SparseCore 0:
  13.8 108.7 all-reduce.5
  128.3 109.3 all-reduce.7
where the time goes:
time: 419 us; the launch traced here: 415 us
  waiting for transfers between devices  187 us (45%)
  other arithmetic  104 us (25%)
  local copies, waits for them, and re-layouts  56.4 us (13%)
  blocking collectives  43 us (10%)
  between operations  14.1 us (3%)
  starting transfers between devices  8.26 us (2%)
    psum x2, waiting for transfers between devices, local(): lax.psum((s_y, s_ty, s_zero, s_one, s_two), 'date')  187 us
    convert_element_type x64, other arithmetic, step(): lax.dynamic_index_in_dim(piece, i, 0, keepdims=True).astype(jnp.float32)  45.1 us
    add x64, other arithmetic, step(): equal = equal + (other == own).astype(jnp.float32)  42.9 us
    all_gather x1, blocking collectives, local(): median = lax.all_gather(part_median, 'date', axis=1, tiled=True)  40.4 us
    unnamed x4, local copies, waits for them, and re-layouts  35 us
    all_to_all x1, local copies, waits for them, and re-layouts, local(): lax.all_to_all(marked, 'date', split_axis=2, concat_axis=0, tiled=True)  12.9 us
    convert_element_type x1, local copies, waits for them, and re-layouts, local(): jnp.where(valid[:, None, :] > 0, values, sentinel).astype(jnp.bfloat16)  8.54 us
  transfers between devices with their start and end apart: 3, of which 2 were waited for; matrix products, arithmetic and copies ran while one was open for 8% of the time, Pallas kernels for 0%

commit v1 on v0

v1 whole, which is shorter than its diff:
```python
import functools

import jax
import jax.numpy as jnp
from jax import lax
from jax.experimental import pallas as pl
from jax.experimental.pallas import tpu as pltpu
from jax.sharding import PartitionSpec as P

ridge = 1.0
sentinel = 100.0
limit = 50.0
big = 1000.0
lanes = 128
gap = 8


def sums_kernel(bands, x_ref, m_ref, out_ref):
    valid = m_ref[...] > 0
    column = lax.broadcasted_iota(jnp.int32, out_ref.shape, 1)
    total = jnp.where(column == bands, jnp.sum(jnp.where(valid, 1.0, 0.0), 1, keepdims=True), 0.0)
    for b in range(bands):
        clear = jnp.where(valid, x_ref[b].astype(jnp.float32), 0.0)
        total += jnp.where(column == b, jnp.sum(clear, 1, keepdims=True), 0.0)
    out_ref[...] = total


def pack_kernel(bands, groups, days_ref, x_ref, m_ref, own_ref, other_ref, out_ref):
    dates, pixels = m_ref.shape
    chunks = out_ref.shape[0]
    width = groups * lanes
    rows = bands * groups * dates
    total = own_ref[...] + other_ref[...]
    column = lax.broadcasted_iota(jnp.int32, total.shape, 1)
    row = lax.broadcasted_iota(jnp.int32, total.shape, 0)
    count = jnp.sum(jnp.where(column == bands, total, 0.0), 1, keepdims=True)
    day = jnp.zeros(total.shape, jnp.float32)
    for d in range(dates):
        day = jnp.where(row == d, days_ref[d].astype(jnp.float32), day)
    stats = jnp.where(column < bands, total / jnp.maximum(count, 1.0), 0.0)
    stats = jnp.where(column == bands, day / 365.0, stats)
    high = stats.astype(jnp.bfloat16).astype(jnp.float32)
    rest = stats - high
    middle = rest.astype(jnp.bfloat16).astype(jnp.float32)
    low = rest - middle
    table = high + pltpu.roll(middle, gap, 1) + pltpu.roll(low, 2 * gap, 1)
    table = table.astype(jnp.bfloat16)
    for c in range(chunks):
        valid = m_ref[:, c * width : (c + 1) * width] > 0
        for b in range(bands):
            value = x_ref[b, :, c * width : (c + 1) * width].astype(jnp.float32)
            marked = jnp.where(valid, value, sentinel).astype(jnp.bfloat16)
            for g in range(groups):
                at = (b * groups + g) * dates
                out_ref[c, at : at + dates, :] = marked[:, g * lanes : (g + 1) * lanes]
        out_ref[c, rows : rows + dates, :] = table


def merge_pairs(n):
    pairs = []

    def merge(lo, length, step):
        jump = step * 2
        if jump < length:
            merge(lo, length, jump)
            merge(lo + step, length, jump)
            for i in range(lo + step, lo + length - step, jump):
                pairs.append((i, i + step))
        else:
            pairs.append((lo, lo + step))

    def sort(lo, length):
        if length > 1:
            half = length // 2
            sort(lo, half)
            sort(lo + half, half)
            merge(lo, length, 1)

    sort(0, n)
    return pairs


def sort_list(items):
    items = list(items)
    n = 1
    while n < len(items):
        n *= 2
    for i, j in merge_pairs(n):
        if j < len(items):
            items[i], items[j] = jnp.minimum(items[i], items[j]), jnp.maximum(items[i], items[j])
    return items


def middle_pair(first, second):
    n = len(first)
    low = [jnp.minimum(first[i], second[n - 1 - i]) for i in range(n)]
    high = [jnp.maximum(first[i], second[n - 1 - i]) for i in range(n)]
    return functools.reduce(jnp.maximum, low), functools.reduce(jnp.minimum, high)


def fit_kernel(bands, groups, dates, in_ref, out_ref, wide_ref, table_ref):
    sources, height, _ = in_ref.shape
    lines = bands * groups
    rows = lines * dates
    pick = lax.broadcasted_iota(jnp.int32, (lanes, (bands + 1) * lanes), 0)
    to = lax.broadcasted_iota(jnp.int32, (lanes, (bands + 1) * lanes), 1) // lanes
    spread = ((pick == to) | (pick == to + gap) | (pick == to + 2 * gap)).astype(jnp.bfloat16)
    for s in range(sources):
        wide_ref[s] = in_ref[s, 0:rows, :].astype(jnp.float32)
    for s in range(sources):
        table_ref[s] = jnp.dot(in_ref[s, rows : rows + dates, :], spread, preferred_element_type=jnp.float32)
    order = [(s, d) for s in range(sources) for d in range(dates)]
    fixed = None
    for start in range(0, lines, 8):
        size = min(8, lines - start)
        shape = (size, lanes)
        line = lax.broadcasted_iota(jnp.int32, shape, 0) + start

        def value_at(s, d):
            return wide_ref[s, pl.ds(start * dates + d, size, stride=dates), :]

        def stat_at(s, d, b):
            return jnp.broadcast_to(table_ref[s, d : d + 1, b * lanes : (b + 1) * lanes], shape)

        def mean_at(s, d):
            mean = stat_at(s, d, start // groups)
            for b in range(start // groups + 1, (start + size - 1) // groups + 1):
                mean = jnp.where(line >= b * groups, stat_at(s, d, b), mean)
            return mean

        sign = jnp.full(shape, big, jnp.float32)
        zero = jnp.zeros(shape, jnp.float32)
        s_y, s_ty = zero, zero
        s_zero, s_one, s_two = zero, zero, zero
        items = []
        for s, d in order:
            value = value_at(s, d)
            clear = value < limit
            items.append(jnp.where(clear, value, sign))
            sign = jnp.where(clear, sign, -sign)
            year = stat_at(s, d, bands)
            part = jnp.where(clear, value - mean_at(s, d), 0.0)
            s_y = s_y + part
            s_ty = s_ty + year * part
            seen = jnp.where(clear, 1.0, 0.0)
            timed = seen * year
            s_zero = s_zero + seen
            s_one = s_one + timed
            s_two = s_two + timed * year
        half = len(items) // 2
        low, high = middle_pair(sort_list(items[:half]), sort_list(items[half:]))
        median = 0.5 * (low + jnp.where(sign > 0, high, low))
        first = s_zero + ridge
        slope = (first * s_ty - s_one * s_y) / (first * (s_two + ridge) - s_one * s_one)
        for c in range(out_ref.shape[0]):
            out_ref[c, start : start + size, :] = median
            out_ref[c, lines + start : lines + start + size, :] = slope


def place_kernel(bands, groups, in_ref, median_ref, slope_ref):
    lines = bands * groups
    for s in range(in_ref.shape[0]):
        for g in range(groups):
            at = (s * groups + g) * lanes
            median_ref[:, at : at + lanes] = in_ref[s, pl.ds(g, bands, stride=groups), :]
            slope_ref[:, at : at + lanes] = in_ref[s, pl.ds(lines + g, bands, stride=groups), :]


def vmem(n):
    return [pl.BlockSpec(memory_space=pltpu.VMEM)] * n


def local(parts, tiles, reflect, cloud_free, days):
    dates, bands, pixels = reflect.shape
    groups = pixels // parts // lanes
    lines = bands * groups
    rows = lines * dates
    height = rows + -(-dates // 8) * 8
    values = jnp.transpose(reflect, (1, 0, 2))
    own = pl.pallas_call(
        functools.partial(sums_kernel, bands),
        out_shape=jax.ShapeDtypeStruct((dates, lanes), jnp.float32),
        in_specs=vmem(2),
        out_specs=vmem(1)[0],
        name="sums",
    )(values, cloud_free)
    if tiles == 2:
        other = lax.ppermute(own, "pix", [(0, 1), (1, 0)])
    else:
        own, other = lax.psum(own, "pix"), jnp.zeros(own.shape, own.dtype)
    packed = pl.pallas_call(
        functools.partial(pack_kernel, bands, groups),
        out_shape=jax.ShapeDtypeStruct((parts, height, lanes), jnp.bfloat16),
        in_specs=[pl.BlockSpec(memory_space=pltpu.SMEM)] + vmem(4),
        out_specs=vmem(1)[0],
        name="pack",
    )(days, values, cloud_free, own, other)
    moved = lax.all_to_all(packed, "date", split_axis=0, concat_axis=0, tiled=True)
    fitted = pl.pallas_call(
        functools.partial(fit_kernel, bands, groups, dates),
        out_shape=jax.ShapeDtypeStruct((parts, 2 * lines, lanes), jnp.float32),
        in_specs=vmem(1),
        out_specs=vmem(1)[0],
        scratch_shapes=[
            pltpu.VMEM((parts, rows, lanes), jnp.float32),
            pltpu.VMEM((parts, dates, (bands + 1) * lanes), jnp.float32),
        ],
        name="fit",
    )(moved)
    spread = lax.all_to_all(fitted, "date", split_axis=0, concat_axis=0, tiled=True)
    shape = jax.ShapeDtypeStruct((bands, pixels), jnp.float32)
    return pl.pallas_call(
        functools.partial(place_kernel, bands, groups),
        out_shape=(shape, shape),
        in_specs=vmem(1),
        out_specs=tuple(vmem(2)),
        name="place",
    )(spread)


def solution(mesh):
    placed = (P("date", None, "pix"), P("date", "pix"), P("date"))
    return jax.shard_map(
        functools.partial(local, mesh.shape["date"], mesh.shape["pix"]),
        mesh=mesh,
        in_specs=placed,
        out_specs=(P(None, "pix"), P(None, "pix")),
        check_vma=False,
    )
```

time: 419 us -> 49.5 us (0.12)
  waiting for transfers between devices: 187 us -> 1.03 us
  other arithmetic: 104 us -> 0 us
  local copies, waits for them, and re-layouts: 56.4 us -> 0.58 us
  between operations: 14.1 us -> 0.63 us
  Pallas kernels: 0 us -> 8.67 us
  starting transfers between devices: 8.26 us -> 0.49 us
  blocking collectives: 43 us -> 37.7 us
    psum x2 -> x0, waiting for transfers between devices: 187 us -> none  [local(): lax.psum((s_y, s_ty, s_zero, s_one, s_two), 'date')]
    convert_element_type x130 -> x0, other arithmetic: 47.5 us -> none  [the longest x64 45.1 us: step(): lax.dynamic_index_in_dim(piece, i, 0, keepdims=True).astype(jnp.float32)]
    add x129 -> x0, other arithmetic: 44.5 us -> none  [the longest x64 42.9 us: step(): equal = equal + (other == own).astype(jnp.float32)]
    all_gather x1 -> x0, blocking collectives: 40.4 us -> none  [local(): median = lax.all_gather(part_median, 'date', axis=1, tiled=True)]
    all_to_all x0 -> x2, blocking collectives: none -> 37.7 us  [the longest x1 21.9 us: local(): lax.all_to_all(packed, 'date', split_axis=0, concat_axis=0, tiled=True)]
    unnamed x4 -> x2, local copies, waits for them, and re-layouts: 35 us -> 0.58 us
    all_to_all x1 -> x0, local copies, waits for them, and re-layouts: 12.9 us -> none  [local(): lax.all_to_all(marked, 'date', split_axis=2, concat_axis=0, tiled=True)]
    pallas_call x0 -> x4, Pallas kernels: none -> 8.67 us  [the longest x1 2.8 us: local(): pl.pallas_call(functools.partial(fit_kernel, bands, groups, dates), out_s...]
  transfers between devices with their start and end apart: 3 -> 1, of which waited for: 2 -> 1; matrix products, arithmetic and copies ran while one was open for 8% -> 0% of each run, Pallas kernels for 0% -> 0%
where the time goes in v1:
time: 49.5 us; the launch traced here: 49.1 us
  blocking collectives  37.7 us (76%)
  Pallas kernels  8.67 us (18%)
  waiting for transfers between devices  1.03 us (2%)
  between operations  0.63 us (1%)
  local copies, waits for them, and re-layouts  0.58 us (1%)
    all_to_all x1, blocking collectives, local(): lax.all_to_all(packed, 'date', split_axis=0, concat_axis=0, tiled=True)  21.9 us
    all_to_all x1, blocking collectives, local(): lax.all_to_all(fitted, 'date', split_axis=0, concat_axis=0, tiled=True)  15.8 us
    pallas_call x1, Pallas kernels, local(): pl.pallas_call(functools.partial(fit_kernel, bands, groups, dates), out_s...  2.8 us
    pallas_call x1, Pallas kernels, local(): pl.pallas_call(functools.partial(pack_kernel, bands, groups), out_shape=j...  2.08 us
    pallas_call x1, Pallas kernels, local(): pl.pallas_call(functools.partial(sums_kernel, bands), out_shape=jax.Shape...  1.93 us
    pallas_call x1, Pallas kernels, local(): pl.pallas_call(functools.partial(place_kernel, bands, groups), out_shape=...  1.85 us
    ppermute x1, waiting for transfers between devices, local(): other = lax.ppermute(own, 'pix', [(0, 1), (1, 0)])  1.03 us
  transfers between devices with their start and end apart: 1, of which 1 were waited for; matrix products, arithmetic and copies ran while one was open for 0% of the time, Pallas kernels for 0%

profile of v1, /device:TPU:0, one launch (start us, length us, event | category | flops | bytes accessed | tf_op | source)
XLA Modules:
  0.0 49.1 jit_solution(1506007101263829332)
XLA Ops:
  0.6 1.9 %sums.1.own_ref = f32[4,128]{1,0:T(4,128)} custom-call(bf16[6,4,8192]{2,1,0:T(4,128)(2,1)} %bitcast.1, s32[4,8192]{1,0:T(4,128)} %m_ref.3), custom_call_target="tpu_custom_call" | custom-call | tf_op jit(solution)/shard_map/sums/pallas_call | solution.py:180
  2.6 0.5 %collective-permute-start = (f32[4,128]{1,0:T(4,128)}, f32[4,128]{1,0:T(4,128)S(1)}, u32[]{:S(2)}, u32[]{:S(2)}) collective-permute-start(f32[4,128]{1,0:T(4,128)} %sums.1.own_ref), channel_id=1, source_target_pairs={{0,1},{1,0},{2,3},{3,2},{4,5},{5,4},{6,7},{7,6},{8,9},{9,8},{10,11... | collective-permute-start | bytes 6152 | tf_op jit(solution)/shard_map/ppermute | solution.py:188
  3.1 1.0 %collective-permute-done.other_ref = f32[4,128]{1,0:T(4,128)S(1)} collective-permute-done((f32[4,128]{1,0:T(4,128)}, f32[4,128]{1,0:T(4,128)S(1)}, u32[]{:S(2)}, u32[]{:S(2)}) %collective-permute-start) | collective-permute-done | bytes 2080 | tf_op jit(solution)/shard_map/ppermute | solution.py:188
  4.1 0.0 copy-start
  4.1 0.6 %copy-done = f32[4,128]{1,0:T(4,128)} copy-done((f32[4,128]{1,0:T(4,128)}, f32[4,128]{1,0:T(4,128)S(1)}, u32[]{:S(2)}) %copy-start) | copy-done | bytes 2072
  4.7 2.1 %pack.1 = bf16[16,104,128]{2,1,0:T(8,128)(2,1)} custom-call(s32[4]{0:T(128)} %days_ref.1, bf16[6,4,8192]{2,1,0:T(4,128)(2,1)} %bitcast.2, s32[4,8192]{1,0:T(4,128)} %m_ref.3, f32[4,128]{1,0:T(4,128)} %sums.1.own_ref, f32[4,128]{1,0:T(4,128)} %copy-done), custom_call_target="tpu_custom_call" | custom-call | tf_op jit(solution)/shard_map/pack/pallas_call | solution.py:191
  6.7 21.9 %all_to_all.10.in_ref = bf16[16,104,128]{2,1,0:T(8,128)(2,1)} all-to-all(bf16[16,104,128]{2,1,0:T(8,128)(2,1)} %pack.1), channel_id=1, replica_groups=mesh['date'=16,'pix'=2] {'date'}, dimensions={0} | all-to-all | bytes 851968 | tf_op jit(solution)/shard_map/all_to_all | solution.py:198
  28.6 2.8 %fit.1 = f32[16,48,128]{2,1,0:T(8,128)} custom-call(bf16[16,104,128]{2,1,0:T(8,128)(2,1)} %all_to_all.10.in_ref), custom_call_target="tpu_custom_call" | custom-call | tf_op jit(solution)/shard_map/fit/pallas_call | solution.py:199
  31.4 15.8 %all_to_all.11.in_ref = f32[16,48,128]{2,1,0:T(8,128)} all-to-all(f32[16,48,128]{2,1,0:T(8,128)} %fit.1), channel_id=1, replica_groups=mesh['date'=16,'pix'=2] {'date'}, dimensions={0} | all-to-all | bytes 786432 | tf_op jit(solution)/shard_map/all_to_all | solution.py:210
  47.2 1.9 %place.1 = (f32[6,8192]{1,0:T(8,128)}, f32[6,8192]{1,0:T(8,128)}) custom-call(f32[16,48,128]{2,1,0:T(8,128)} %all_to_all.11.in_ref), custom_call_target="tpu_custom_call" | custom-call | tf_op jit(solution)/shard_map/place/pallas_call | solution.py:212
Async XLA Ops:
  2.6 1.5 %collective-permute-start = (f32[4,128]{1,0:T(4,128)}, f32[4,128]{1,0:T(4,128)S(1)}, u32[]{:S(2)}, u32[]{:S(2)}) collective-permute-start(f32[4,128]{1,0:T(4,128)} %sums.1.own_ref), channel_id=1, source_target_pairs={{0,1},{1,0},{2,3},{3,2},{4,5},{5,4},{6,7},{7,6},{8,9},{9,8},{10,11... | collective-permute-start | bytes 6152 | tf_op jit(solution)/shard_map/ppermute | solution.py:188
  4.1 0.6 %copy-start = (f32[4,128]{1,0:T(4,128)}, f32[4,128]{1,0:T(4,128)S(1)}, u32[]{:S(2)}) copy-start(f32[4,128]{1,0:T(4,128)S(1)} %collective-permute-done.other_ref) | copy-start | bytes 6148

commit v2 on v1

v2 whole, which is shorter than its diff:
```python
import functools

import jax
import jax.numpy as jnp
from jax import lax
from jax.experimental import pallas as pl
from jax.experimental.pallas import tpu as pltpu
from jax.sharding import PartitionSpec as P

ridge = 1.0
sentinel = 100.0
limit = 50.0
big = 1000.0
lanes = 128
order = (6, 7, 11, 5, 15, 10, 14, 13, 12, 3, 1, 9, 8, 4, 0, 2)


def split_pieces(table, gap):
    high = table.astype(jnp.bfloat16).astype(jnp.float32)
    rest = table - high
    middle = rest.astype(jnp.bfloat16).astype(jnp.float32)
    low = rest - middle
    return (high + pltpu.roll(middle, gap, 1) + pltpu.roll(low, 2 * gap, 1)).astype(jnp.bfloat16)


def pack_kernel(bands, groups, days_ref, x_hbm, m_hbm, out_ref, x_ref, m_ref, sems):
    dates, _ = m_ref.shape
    chunks = out_ref.shape[0]
    width = groups * lanes
    rows = bands * groups * dates
    mask_copy = pltpu.make_async_copy(m_hbm, m_ref, sems.at[bands])
    mask_copy.start()
    copies = [pltpu.make_async_copy(x_hbm.at[b], x_ref.at[b], sems.at[b]) for b in range(bands)]
    for copy in copies:
        copy.start()
    shape = (dates, lanes)
    column = lax.broadcasted_iota(jnp.int32, shape, 1)
    row = lax.broadcasted_iota(jnp.int32, shape, 0)
    day = jnp.zeros(shape, jnp.float32)
    for d in range(dates):
        day = jnp.where(row == d, days_ref[d].astype(jnp.float32), day)
    mask_copy.wait()
    count = jnp.sum(jnp.where(m_ref[...] > 0, 1.0, 0.0), 1, keepdims=True)
    table = jnp.where(column == bands, count, jnp.where(column == bands + 1, day, 0.0))
    for b in range(bands):
        copies[b].wait()
        total = jnp.zeros((dates, width), jnp.float32)
        for c in range(chunks):
            valid = m_ref[:, c * width : (c + 1) * width] > 0
            value = x_ref[b, :, c * width : (c + 1) * width].astype(jnp.float32)
            total += jnp.where(valid, value, 0.0)
            marked = jnp.where(valid, value, sentinel).astype(jnp.bfloat16)
            for g in range(groups):
                at = (b * groups + g) * dates
                out_ref[c, at : at + dates, :] = marked[:, g * lanes : (g + 1) * lanes]
        table = jnp.where(column == b, jnp.sum(total, 1, keepdims=True), table)
    table = split_pieces(jnp.where(column < bands + 2, table, 0.0), bands + 2)
    for c in range(chunks):
        out_ref[c, rows : rows + dates, :] = table


def stats_kernel(gap, rows, in_ref, out_ref):
    dates = out_ref.shape[0] // in_ref.shape[0]
    for s in range(in_ref.shape[0]):
        part = in_ref[s, rows : rows + dates, :].astype(jnp.float32)
        part = part + pltpu.roll(part, lanes - gap, 1) + pltpu.roll(part, lanes - 2 * gap, 1)
        out_ref[s * dates : (s + 1) * dates, :] = part


def merge_pairs(n):
    pairs = []

    def merge(lo, length, step):
        jump = step * 2
        if jump < length:
            merge(lo, length, jump)
            merge(lo + step, length, jump)
            for i in range(lo + step, lo + length - step, jump):
                pairs.append((i, i + step))
        else:
            pairs.append((lo, lo + step))

    def sort(lo, length):
        if length > 1:
            half = length // 2
            sort(lo, half)
            sort(lo + half, half)
            merge(lo, length, 1)

    sort(0, n)
    return pairs


def sort_list(items):
    items = list(items)
    n = 1
    while n < len(items):
        n *= 2
    for i, j in merge_pairs(n):
        if j < len(items):
            items[i], items[j] = jnp.minimum(items[i], items[j]), jnp.maximum(items[i], items[j])
    return items


def middle_pair(first, second):
    n = len(first)
    low = [jnp.minimum(first[i], second[n - 1 - i]) for i in range(n)]
    high = [jnp.maximum(first[i], second[n - 1 - i]) for i in range(n)]
    return functools.reduce(jnp.maximum, low), functools.reduce(jnp.minimum, high)


def blocks_of(lines):
    return [(start, min(8, lines - start)) for start in range(0, lines, 8)]


def median_kernel(lines, dates, in_ref, out_ref, wide_ref):
    sources = in_ref.shape[0]
    rows = lines * dates
    for s in range(sources):
        wide_ref[s] = in_ref[s, 0:rows, :].astype(jnp.float32)
    for start, size in blocks_of(lines):
        sign = jnp.full((size, lanes), big, jnp.float32)
        items = []
        for s in range(sources):
            for d in range(dates):
                value = wide_ref[s, pl.ds(start * dates + d, size, stride=dates), :]
                clear = value < limit
                items.append(jnp.where(clear, value, sign))
                sign = jnp.where(clear, sign, -sign)
        half = len(items) // 2
        low, high = middle_pair(sort_list(items[:half]), sort_list(items[half:]))
        out_ref[start : start + size, :] = 0.5 * (low + jnp.where(sign > 0, high, low))


def slope_kernel(bands, groups, wide_ref, own_ref, other_ref, median_ref, out_ref, table_ref):
    sources, rows, _ = wide_ref.shape
    lines = bands * groups
    dates = rows // lines
    gap = bands + 2
    own = own_ref[...]
    total = own + other_ref[...]
    column = lax.broadcasted_iota(jnp.int32, total.shape, 1)
    count = jnp.sum(jnp.where(column == bands, total, 0.0), 1, keepdims=True)
    stats = jnp.where(column < bands, total / jnp.maximum(count, 1.0), 0.0)
    stats = jnp.where(column == bands + 1, own / 365.0, stats)
    pick = lax.broadcasted_iota(jnp.int32, (lanes, (bands + 1) * lanes), 0)
    to = lax.broadcasted_iota(jnp.int32, (lanes, (bands + 1) * lanes), 1) // lanes
    to = jnp.where(to == bands, bands + 1, to)
    spread = ((pick == to) | (pick == to + gap) | (pick == to + 2 * gap)).astype(jnp.bfloat16)
    table_ref[...] = jnp.dot(split_pieces(stats, gap), spread, preferred_element_type=jnp.float32)
    shared = None
    for start, size in blocks_of(lines):
        shape = (size, lanes)
        line = lax.broadcasted_iota(jnp.int32, shape, 0) + start
        fresh = shared is None or 8 % groups != 0 or shared[0].shape != shape
        zero = jnp.zeros(shape, jnp.float32)
        s_y, s_ty, s_zero, s_one, s_two = zero, zero, zero, zero, zero
        for s in range(sources):
            for d in range(dates):
                at = s * dates + d

                def stat_at(b):
                    row = table_ref[at : at + 1, b * lanes : (b + 1) * lanes]
                    return jnp.broadcast_to(row, shape)

                mean = stat_at(start // groups)
                for b in range(start // groups + 1, (start + size - 1) // groups + 1):
                    mean = jnp.where(line >= b * groups, stat_at(b), mean)
                value = wide_ref[s, pl.ds(start * dates + d, size, stride=dates), :]
                clear = value < limit
                year = stat_at(bands)
                part = jnp.where(clear, value - mean, 0.0)
                s_y = s_y + part
                s_ty = s_ty + year * part
                if fresh:
                    timed = jnp.where(clear, year, 0.0)
                    s_zero = s_zero + jnp.where(clear, 1.0, 0.0)
                    s_one = s_one + timed
                    s_two = s_two + timed * year
        if fresh:
            first = s_zero + ridge
            shared = (first, s_one, first * (s_two + ridge) - s_one * s_one)
        first, s_one, determinant = shared
        slope = (first * s_ty - s_one * s_y) / determinant
        for c in range(out_ref.shape[0]):
            out_ref[c, start : start + size, :] = median_ref[start : start + size, :]
            out_ref[c, lines + start : lines + start + size, :] = slope


def place_kernel(bands, groups, in_ref, median_ref, slope_ref):
    lines = bands * groups
    for s in range(in_ref.shape[0]):
        for g in range(groups):
            at = (s * groups + g) * lanes
            median_ref[:, at : at + lanes] = in_ref[s, pl.ds(g, bands, stride=groups), :]
            slope_ref[:, at : at + lanes] = in_ref[s, pl.ds(lines + g, bands, stride=groups), :]


def call(kernel, name, out_shape, in_specs, scratch=(), flops=0):
    many = isinstance(out_shape, tuple)
    spec = pl.BlockSpec(memory_space=pltpu.VMEM)
    cost = pl.CostEstimate(flops=flops, bytes_accessed=flops, transcendentals=0) if flops else None
    return pl.pallas_call(
        kernel,
        out_shape=out_shape,
        in_specs=[pl.BlockSpec(memory_space=space) for space in in_specs],
        out_specs=tuple([spec] * len(out_shape)) if many else spec,
        scratch_shapes=scratch,
        compiler_params=pltpu.CompilerParams(vmem_limit_bytes=8 * 1024 * 1024),
        cost_estimate=cost,
        name=name,
    )


def exchange(x):
    groups = [list(order)] if len(order) == x.shape[0] else None
    return lax.all_to_all(x, "date", split_axis=0, concat_axis=0, tiled=True, axis_index_groups=groups)


def local(parts, tiles, reflect, cloud_free, days):
    dates, bands, pixels = reflect.shape
    groups = pixels // parts // lanes
    lines = bands * groups
    rows = lines * dates
    height = rows + -(-dates // 8) * 8
    inside, outside = pltpu.VMEM, pltpu.HBM
    array = jax.ShapeDtypeStruct
    values = jnp.transpose(reflect, (1, 0, 2))
    packed = call(
        functools.partial(pack_kernel, bands, groups),
        "pack",
        array((parts, height, lanes), jnp.bfloat16),
        [pltpu.SMEM, outside, outside],
        [
            pltpu.VMEM((bands, dates, pixels), jnp.bfloat16),
            pltpu.VMEM((dates, pixels), jnp.int32),
            pltpu.SemaphoreType.DMA((bands + 1,)),
        ],
    )(*[pltpu.with_memory_space_constraint(x, outside) if x.size > 1 else x for x in (days, values, cloud_free)])
    moved = exchange(packed)
    own = call(
        functools.partial(stats_kernel, bands + 2, rows),
        "stats",
        array((parts * dates, lanes), jnp.float32),
        [inside],
    )(moved)
    if tiles == 2:
        other = lax.ppermute(own, "pix", [(0, 1), (1, 0)])
    else:
        ring = [(i, (i + 1) % tiles) for i in range(tiles)]
        passed, other = own, jnp.zeros(own.shape, own.dtype)
        for _ in range(tiles - 1):
            passed = lax.ppermute(passed, "pix", ring)
            other = other + passed
    median, wide = call(
        functools.partial(median_kernel, lines, dates),
        "median",
        (array((lines, lanes), jnp.float32), array((parts, rows, lanes), jnp.float32)),
        [inside],
        flops=16_000_000,
    )(moved)
    fitted = call(
        functools.partial(slope_kernel, bands, groups),
        "slope",
        array((parts, 2 * lines, lanes), jnp.float32),
        [inside] * 4,
        [pltpu.VMEM((parts * dates, (bands + 1) * lanes), jnp.float32)],
    )(wide, own, other, median)
    spread = exchange(fitted)
    shape = array((bands, pixels), jnp.float32)
    return call(functools.partial(place_kernel, bands, groups), "place", (shape, shape), [inside])(spread)


def solution(mesh):
    placed = (P("date", None, "pix"), P("date", "pix"), P("date"))
    return jax.shard_map(
        functools.partial(local, mesh.shape["date"], mesh.shape["pix"]),
        mesh=mesh,
        in_specs=placed,
        out_specs=(P(None, "pix"), P(None, "pix")),
        check_vma=False,
    )
```

time: 49.5 us -> 41.1 us (0.83)
  Pallas kernels: 8.67 us -> 4.72 us
  blocking collectives: 37.7 us -> 34.8 us
  local copies, waits for them, and re-layouts: 0.58 us -> 0 us
    pallas_call x4 -> x5, Pallas kernels: 8.67 us -> 4.72 us  [the longest x1 2.59 us: local(): call(functools.partial(pack_kernel, bands, groups), 'pack', array((parts,...]
    all_to_all x2, blocking collectives: 37.7 us -> 34.8 us  [exchange(): lax.all_to_all(x, 'date', split_axis=0, concat_axis=0, tiled=True, axis_i...]
    unnamed x2 -> x0, local copies, waits for them, and re-layouts: 0.58 us -> none
  transfers between devices with their start and end apart: 1 -> 1, of which waited for: 1 -> 1; matrix products, arithmetic and copies ran while one was open for 0% -> 0% of each run, Pallas kernels for 0% -> 1%
where the time goes in v2:
time: 41.1 us; the launch traced here: 40.9 us
  blocking collectives  34.8 us (85%)
  Pallas kernels  4.72 us (11%)
  between operations  0.66 us (2%)
  waiting for transfers between devices  0.64 us (2%)
    all_to_all x2, blocking collectives, exchange(): lax.all_to_all(x, 'date', split_axis=0, concat_axis=0, tiled=True, axis_i...  34.8 us
    pallas_call x1, Pallas kernels, local(): call(functools.partial(pack_kernel, bands, groups), 'pack', array((parts,...  2.59 us
    pallas_call x1, Pallas kernels, local(): call(functools.partial(place_kernel, bands, groups), 'place', (shape, sha...  0.86 us
  transfers between devices with their start and end apart: 1, of which 1 were waited for; matrix products, arithmetic and copies ran while one was open for 0% of the time, Pallas kernels for 1%

profile of v2, /device:TPU:0, one launch (start us, length us, event | category | flops | bytes accessed | tf_op | source)
XLA Modules:
  0.0 40.9 jit_solution(11652839571410224634)
XLA Ops:
  0.6 2.6 %pack.1 = bf16[16,104,128]{2,1,0:T(8,128)(2,1)S(1)} custom-call(s32[4]{0:T(128)} %days_ref.1, bf16[6,4,8192]{2,1,0:T(4,128)(2,1)} %bitcast.1, s32[4,8192]{1,0:T(4,128)} %m_hbm.1), custom_call_target="tpu_custom_call" | custom-call | tf_op jit(solution)/shard_map/pack/pallas_call | solution.py:229
  3.2 19.6 %all_to_all.10.in_ref = bf16[16,104,128]{2,1,0:T(8,128)(2,1)S(1)} all-to-all(bf16[16,104,128]{2,1,0:T(8,128)(2,1)S(1)} %pack.1), channel_id=1, replica_groups={{12,14,22,10,30,20,28,26,24,6,2,18,16,8,0,4},{13,15,23,11,31,21,29,27,2..., dimensions={0} | all-to-all | bytes 851968 | tf_op jit(solution)/shard_map/all_to_all | solution.py:217
  22.8 0.1 stats.1.own_ref
  22.9 0.1 collective-permute-start
  23.0 0.6 %median.1 = (f32[24,128]{1,0:T(8,128)S(1)}, f32[16,96,128]{2,1,0:T(8,128)S(1)}) custom-call(bf16[16,104,128]{2,1,0:T(8,128)(2,1)S(1)} %all_to_all.10.in_ref), custom_call_target="tpu_custom_call" | custom-call | flops 16000000 | bytes 16000000 | tf_op jit(solution)/shard_map/median/pallas_call | solution.py:255
  23.5 0.6 %collective-permute-done.other_ref = f32[64,128]{1,0:T(8,128)S(1)} collective-permute-done((f32[64,128]{1,0:T(8,128)S(1)}, f32[64,128]{1,0:T(8,128)S(1)}, u32[]{:S(2)}, u32[]{:S(2)}) %collective-permute-start) | collective-permute-done | bytes 32800 | tf_op jit(solution)/shard_map/ppermute | solution.py:248
  24.2 0.6 %slope.1 = f32[16,48,128]{2,1,0:T(8,128)S(1)} custom-call(f32[16,96,128]{2,1,0:T(8,128)S(1)} %get-tuple-element.4.wide_ref, f32[64,128]{1,0:T(8,128)S(1)} %stats.1.own_ref, f32[64,128]{1,0:T(8,128)S(1)} %collective-permute-done.other_ref, f32[24,128]{1,0:T(8,128)S(1)} %get-tuple-element.5.median_ref), custom_call_target="tpu_custom_call" | custom-call | tf_op jit(solution)/shard_map/slope/pallas_call | solution.py:262
  24.8 15.2 %all_to_all.11.in_ref = f32[16,48,128]{2,1,0:T(8,128)S(1)} all-to-all(f32[16,48,128]{2,1,0:T(8,128)S(1)} %slope.1), channel_id=1, replica_groups={{12,14,22,10,30,20,28,26,24,6,2,18,16,8,0,4},{13,15,23,11,31,21,29,27,2..., dimensions={0} | all-to-all | bytes 786432 | tf_op jit(solution)/shard_map/all_to_all | solution.py:217
  40.0 0.9 %place.1 = (f32[6,8192]{1,0:T(8,128)}, f32[6,8192]{1,0:T(8,128)}) custom-call(f32[16,48,128]{2,1,0:T(8,128)S(1)} %all_to_all.11.in_ref), custom_call_target="tpu_custom_call" | custom-call | tf_op jit(solution)/shard_map/place/pallas_call | solution.py:271
Async XLA Ops:
  22.9 1.3 %collective-permute-start = (f32[64,128]{1,0:T(8,128)S(1)}, f32[64,128]{1,0:T(8,128)S(1)}, u32[]{:S(2)}, u32[]{:S(2)}) collective-permute-start(f32[64,128]{1,0:T(8,128)S(1)} %stats.1.own_ref), channel_id=1, source_target_pairs={{0,1},{1,0},{2,3},{3,2},{4,5},{5,4},{6,7},{7,6},{8,9},{9,8},{10,11... | collective-permute-start | bytes 98312 | tf_op jit(solution)/shard_map/ppermute | solution.py:248

commit v3 on v2

v3 whole, which is shorter than its diff:
```python
import functools

import jax
import jax.numpy as jnp
from jax import lax
from jax.experimental import pallas as pl
from jax.experimental.pallas import tpu as pltpu
from jax.sharding import PartitionSpec as P

ridge = 1.0
sentinel = 100.0
limit = 50.0
big = 1000.0
lanes = 128
order = (6, 7, 11, 5, 15, 10, 14, 13, 12, 3, 1, 9, 8, 4, 0, 2)


def split_pieces(table, gap):
    high = table.astype(jnp.bfloat16).astype(jnp.float32)
    rest = table - high
    middle = rest.astype(jnp.bfloat16).astype(jnp.float32)
    low = rest - middle
    return (high + pltpu.roll(middle, gap, 1) + pltpu.roll(low, 2 * gap, 1)).astype(jnp.bfloat16)


def load_kernel(bands, d_hbm, x_hbm, m_hbm, x_ref, m_ref, out_ref, days_ref, sems):
    dates, pixels = m_ref.shape
    mask_copy = pltpu.make_async_copy(m_hbm, m_ref, sems.at[0])
    mask_copy.start()
    value_copy = pltpu.make_async_copy(x_hbm, x_ref, sems.at[1])
    value_copy.start()
    days_copy = pltpu.make_async_copy(d_hbm, days_ref, sems.at[2])
    days_copy.start()
    shape = (dates, lanes)
    column = lax.broadcasted_iota(jnp.int32, shape, 1)
    row = lax.broadcasted_iota(jnp.int32, shape, 0)
    tiles = [slice(at, at + lanes) for at in range(0, pixels, lanes)]
    mask_copy.wait()
    totals = [sum(jnp.where(m_ref[:, at] > 0, 1.0, 0.0) for at in tiles)]
    value_copy.wait()
    for b in range(bands):
        totals.append(sum(jnp.where(m_ref[:, at] > 0, x_ref[b, :, at].astype(jnp.float32), 0.0) for at in tiles))
    table = jnp.zeros(shape, jnp.float32)
    days_copy.wait()
    for d in range(dates):
        table = jnp.where((row == d) & (column == bands + 1), days_ref[d].astype(jnp.float32), table)
    for b, total in enumerate(totals[1:] + totals[:1]):
        table = jnp.where(column == b, jnp.sum(total, 1, keepdims=True), table)
    out_ref[...] = table


def pack_kernel(bands, groups, x_ref, m_ref, out_ref):
    dates, _ = m_ref.shape
    width = groups * lanes
    for c in range(out_ref.shape[0]):
        valid = m_ref[:, c * width : (c + 1) * width] > 0
        for b in range(bands):
            value = x_ref[b, :, c * width : (c + 1) * width].astype(jnp.float32)
            marked = jnp.where(valid, value, sentinel).astype(jnp.bfloat16)
            for g in range(groups):
                at = (b * groups + g) * dates
                out_ref[c, at : at + dates, :] = marked[:, g * lanes : (g + 1) * lanes]


def stamp_kernel(bands, rows, own_ref, other_ref, in_ref, out_ref):
    del in_ref
    own = own_ref[...]
    total = own + other_ref[...]
    dates = total.shape[0]
    column = lax.broadcasted_iota(jnp.int32, total.shape, 1)
    count = jnp.sum(jnp.where(column == bands, total, 0.0), 1, keepdims=True)
    stats = jnp.where(column < bands, total / jnp.maximum(count, 1.0), 0.0)
    stats = split_pieces(jnp.where(column == bands + 1, own / 365.0, stats), bands + 2)
    for c in range(out_ref.shape[0]):
        out_ref[c, rows : rows + dates, :] = stats


def merge_pairs(n):
    pairs = []

    def merge(lo, length, step):
        jump = step * 2
        if jump < length:
            merge(lo, length, jump)
            merge(lo + step, length, jump)
            for i in range(lo + step, lo + length - step, jump):
                pairs.append((i, i + step))
        else:
            pairs.append((lo, lo + step))

    def sort(lo, length):
        if length > 1:
            half = length // 2
            sort(lo, half)
            sort(lo + half, half)
            merge(lo, length, 1)

    sort(0, n)
    return pairs


def sort_list(items):
    items = list(items)
    n = 1
    while n < len(items):
        n *= 2
    for i, j in merge_pairs(n):
        if j < len(items):
            items[i], items[j] = jnp.minimum(items[i], items[j]), jnp.maximum(items[i], items[j])
    return items


def middle_pair(first, second):
    n = len(first)
    low = [jnp.minimum(first[i], second[n - 1 - i]) for i in range(n)]
    high = [jnp.maximum(first[i], second[n - 1 - i]) for i in range(n)]
    return functools.reduce(jnp.maximum, low), functools.reduce(jnp.minimum, high)


def blocks_of(lines):
    return [(start, min(8, lines - start)) for start in range(0, lines, 8)]


def fit_kernel(bands, groups, dates, in_ref, out_ref, wide_ref, table_ref):
    sources = in_ref.shape[0]
    lines = bands * groups
    rows = lines * dates
    gap = bands + 2
    wide = (lanes, (bands + 1) * lanes)
    pick = lax.broadcasted_iota(jnp.int32, wide, 0)
    to = lax.broadcasted_iota(jnp.int32, wide, 1) // lanes
    to = jnp.where(to == bands, bands + 1, to)
    spread = ((pick == to) | (pick == to + gap) | (pick == to + 2 * gap)).astype(jnp.bfloat16)
    for s in range(sources):
        wide_ref[s] = in_ref[s, 0:rows, :].astype(jnp.float32)
        table_ref[s] = jnp.dot(in_ref[s, rows : rows + dates, :], spread, preferred_element_type=jnp.float32)
    shared = None
    for start, size in blocks_of(lines):
        shape = (size, lanes)
        line = lax.broadcasted_iota(jnp.int32, shape, 0) + start
        fresh = shared is None or 8 % groups != 0 or shared[0].shape != shape
        zero = jnp.zeros(shape, jnp.float32)
        sign = jnp.full(shape, big, jnp.float32)
        s_y, s_ty, s_zero, s_one, s_two = zero, zero, zero, zero, zero
        items = []
        for s in range(sources):
            for d in range(dates):

                def stat_at(b):
                    row = table_ref[s, d : d + 1, b * lanes : (b + 1) * lanes]
                    return jnp.broadcast_to(row, shape)

                mean = stat_at(start // groups)
                for b in range(start // groups + 1, (start + size - 1) // groups + 1):
                    mean = jnp.where(line >= b * groups, stat_at(b), mean)
                value = wide_ref[s, pl.ds(start * dates + d, size, stride=dates), :]
                clear = value < limit
                items.append(jnp.where(clear, value, sign))
                sign = jnp.where(clear, sign, -sign)
                year = stat_at(bands)
                part = jnp.where(clear, value - mean, 0.0)
                s_y = s_y + part
                s_ty = s_ty + year * part
                if fresh:
                    timed = jnp.where(clear, year, 0.0)
                    s_zero = s_zero + jnp.where(clear, 1.0, 0.0)
                    s_one = s_one + timed
                    s_two = s_two + timed * year
        half = len(items) // 2
        low, high = middle_pair(sort_list(items[:half]), sort_list(items[half:]))
        median = 0.5 * (low + jnp.where(sign > 0, high, low))
        if fresh:
            first = s_zero + ridge
            shared = (first, s_one, first * (s_two + ridge) - s_one * s_one)
        first, s_one, determinant = shared
        slope = (first * s_ty - s_one * s_y) / determinant
        for c in range(out_ref.shape[0]):
            out_ref[c, start : start + size, :] = median
            out_ref[c, lines + start : lines + start + size, :] = slope


def place_kernel(bands, groups, in_ref, median_ref, slope_ref):
    lines = bands * groups
    for s in range(in_ref.shape[0]):
        for g in range(groups):
            at = (s * groups + g) * lanes
            median_ref[:, at : at + lanes] = in_ref[s, pl.ds(g, bands, stride=groups), :]
            slope_ref[:, at : at + lanes] = in_ref[s, pl.ds(lines + g, bands, stride=groups), :]


def call(kernel, name, out_shape, in_specs, scratch=(), flops=0, aliases={}):
    many = isinstance(out_shape, tuple)
    spec = pl.BlockSpec(memory_space=pltpu.VMEM)
    cost = pl.CostEstimate(flops=flops, bytes_accessed=flops, transcendentals=0) if flops else None
    return pl.pallas_call(
        kernel,
        out_shape=out_shape,
        in_specs=[pl.BlockSpec(memory_space=space) for space in in_specs],
        out_specs=tuple([spec] * len(out_shape)) if many else spec,
        scratch_shapes=scratch,
        compiler_params=pltpu.CompilerParams(vmem_limit_bytes=8 * 1024 * 1024),
        cost_estimate=cost,
        input_output_aliases=aliases,
        name=name,
    )


def exchange(x):
    groups = [list(order)] if len(order) == x.shape[0] else None
    return lax.all_to_all(x, "date", split_axis=0, concat_axis=0, tiled=True, axis_index_groups=groups)


def local(parts, tiles, reflect, cloud_free, days):
    dates, bands, pixels = reflect.shape
    groups = pixels // parts // lanes
    lines = bands * groups
    rows = lines * dates
    height = rows + -(-dates // 8) * 8
    inside, outside = pltpu.VMEM, pltpu.HBM
    array = jax.ShapeDtypeStruct
    values = jnp.transpose(reflect, (1, 0, 2))
    held, mask, own = call(
        functools.partial(load_kernel, bands),
        "load",
        (
            array(values.shape, values.dtype),
            array(cloud_free.shape, cloud_free.dtype),
            array((dates, lanes), jnp.float32),
        ),
        [outside if dates > 1 else pl.ANY, outside, outside],
        [pltpu.SMEM((dates,), jnp.int32), pltpu.SemaphoreType.DMA((3,))],
    )(*[pltpu.with_memory_space_constraint(x, outside) if x.size > 1 else x for x in (days, values, cloud_free)])
    if tiles == 2:
        other = lax.ppermute(own, "pix", [(0, 1), (1, 0)])
    else:
        ring = [(i, (i + 1) % tiles) for i in range(tiles)]
        passed, other = own, jnp.zeros(own.shape, own.dtype)
        for _ in range(tiles - 1):
            passed = lax.ppermute(passed, "pix", ring)
            other = other + passed
    packed = call(
        functools.partial(pack_kernel, bands, groups),
        "pack",
        array((parts, height, lanes), jnp.bfloat16),
        [inside, inside],
        flops=16_000_000,
    )(held, mask)
    stamped = call(
        functools.partial(stamp_kernel, bands, rows),
        "stamp",
        array(packed.shape, packed.dtype),
        [inside] * 3,
        aliases={2: 0},
    )(own, other, pltpu.with_memory_space_constraint(packed, inside))
    moved = exchange(stamped)
    fitted = call(
        functools.partial(fit_kernel, bands, groups, dates),
        "fit",
        array((parts, 2 * lines, lanes), jnp.float32),
        [inside],
        [
            pltpu.VMEM((parts, rows, lanes), jnp.float32),
            pltpu.VMEM((parts, dates, (bands + 1) * lanes), jnp.float32),
        ],
    )(moved)
    spread = exchange(fitted)
    shape = array((bands, pixels), jnp.float32)
    return call(functools.partial(place_kernel, bands, groups), "place", (shape, shape), [inside])(spread)


def solution(mesh):
    placed = (P("date", None, "pix"), P("date", "pix"), P("date"))
    return jax.shard_map(
        functools.partial(local, mesh.shape["date"], mesh.shape["pix"]),
        mesh=mesh,
        in_specs=placed,
        out_specs=(P(None, "pix"), P(None, "pix")),
        check_vma=False,
    )
```

time: 41.1 us -> 38.9 us (0.946)
  blocking collectives: 34.8 us -> 33.3 us
  Pallas kernels: 4.72 us -> 3.53 us
  starting transfers between devices: 0.07 us -> 0.56 us
    pallas_call x1, Pallas kernels: 2.59 us -> 0.16 us  [local(): call(functools.partial(pack_kernel, bands, groups), 'pack', array((parts,...]
    all_to_all x2, blocking collectives: 34.8 us -> 33.3 us  [exchange(): lax.all_to_all(x, 'date', split_axis=0, concat_axis=0, tiled=True, axis_i...]
    pallas_call x3, Pallas kernels: 1.27 us -> 2.51 us  [the longest x1 1.41 us: local(): call(functools.partial(load_kernel, bands), 'load', (array(values.shape,...]
    ppermute x1, starting transfers between devices: 0.07 us -> 0.56 us  [local(): other = lax.ppermute(own, 'pix', [(0, 1), (1, 0)])]
  transfers between devices with their start and end apart: 1 -> 1, of which waited for: 1 -> 1; matrix products, arithmetic and copies ran while one was open for 0% -> 0% of each run, Pallas kernels for 1% -> 0%
where the time goes in v3:
time: 38.9 us; the launch traced here: 38.7 us
  blocking collectives  33.3 us (86%)
  Pallas kernels  3.53 us (9%)
  waiting for transfers between devices  0.66 us (2%)
  between operations  0.65 us (2%)
  starting transfers between devices  0.56 us (1%)
    all_to_all x2, blocking collectives, exchange(): lax.all_to_all(x, 'date', split_axis=0, concat_axis=0, tiled=True, axis_i...  33.3 us
    pallas_call x1, Pallas kernels, local(): call(functools.partial(load_kernel, bands), 'load', (array(values.shape,...  1.41 us
    pallas_call x1, Pallas kernels, local(): call(functools.partial(fit_kernel, bands, groups, dates), 'fit', array((p...  0.94 us
    pallas_call x1, Pallas kernels, local(): call(functools.partial(place_kernel, bands, groups), 'place', (shape, sha...  0.86 us
  transfers between devices with their start and end apart: 1, of which 1 were waited for; matrix products, arithmetic and copies ran while one was open for 0% of the time, Pallas kernels for 0%

profile of v3, /device:TPU:0, one launch (start us, length us, event | category | flops | bytes accessed | tf_op | source)
XLA Modules:
  0.0 38.7 jit_solution(1930707827922002763)
XLA Ops:
  0.6 1.4 %load.1 = (bf16[6,4,8192]{2,1,0:T(4,128)(2,1)S(1)}, s32[4,8192]{1,0:T(4,128)S(1)}, f32[4,128]{1,0:T(4,128)S(1)}) custom-call(s32[4]{0:T(128)} %d_hbm.1, bf16[6,4,8192]{2,1,0:T(4,128)(2,1)} %bitcast.1, s32[4,8192]{1,0:T(4,128)} %m_hbm.1), custom_call_target="tpu_custom_call" | custom-call | tf_op jit(solution)/shard_map/load/pallas_call | solution.py:222
  2.0 0.6 %collective-permute-start = (f32[4,128]{1,0:T(4,128)S(1)}, f32[4,128]{1,0:T(4,128)S(1)}, u32[]{:S(2)}, u32[]{:S(2)}) collective-permute-start(f32[4,128]{1,0:T(4,128)S(1)} %get-tuple-element.5.own_ref), channel_id=1, source_target_pairs={{0,1},{1,0},{2,3},{3,2},{4,5},{5,4},{6,7},{7,6},{8,9},{9,8},{10,11... | collective-permute-start | bytes 6152 | tf_op jit(solution)/shard_map/ppermute | solution.py:234
  2.6 0.2 pack.1.in_ref
  2.8 0.7 %collective-permute-done.other_ref = f32[4,128]{1,0:T(4,128)S(1)} collective-permute-done((f32[4,128]{1,0:T(4,128)S(1)}, f32[4,128]{1,0:T(4,128)S(1)}, u32[]{:S(2)}, u32[]{:S(2)}) %collective-permute-start) | collective-permute-done | bytes 2080 | tf_op jit(solution)/shard_map/ppermute | solution.py:234
  3.4 0.2 stamp.1
  3.6 19.7 %all_to_all.10.in_ref = bf16[16,104,128]{2,1,0:T(8,128)(2,1)S(1)} all-to-all(bf16[16,104,128]{2,1,0:T(8,128)(2,1)S(1)} %stamp.1), channel_id=1, replica_groups={{12,14,22,10,30,20,28,26,24,6,2,18,16,8,0,4},{13,15,23,11,31,21,29,27,2..., dimensions={0} | all-to-all | bytes 851968 | tf_op jit(solution)/shard_map/all_to_all | solution.py:210
  23.3 0.9 %fit.1 = f32[16,48,128]{2,1,0:T(8,128)S(1)} custom-call(bf16[16,104,128]{2,1,0:T(8,128)(2,1)S(1)} %all_to_all.10.in_ref), custom_call_target="tpu_custom_call" | custom-call | tf_op jit(solution)/shard_map/fit/pallas_call | solution.py:256
  24.3 13.5 %all_to_all.11.in_ref = f32[16,48,128]{2,1,0:T(8,128)S(1)} all-to-all(f32[16,48,128]{2,1,0:T(8,128)S(1)} %fit.1), channel_id=1, replica_groups={{12,14,22,10,30,20,28,26,24,6,2,18,16,8,0,4},{13,15,23,11,31,21,29,27,2..., dimensions={0} | all-to-all | bytes 786432 | tf_op jit(solution)/shard_map/all_to_all | solution.py:210
  37.8 0.9 %place.1 = (f32[6,8192]{1,0:T(8,128)}, f32[6,8192]{1,0:T(8,128)}) custom-call(f32[16,48,128]{2,1,0:T(8,128)S(1)} %all_to_all.11.in_ref), custom_call_target="tpu_custom_call" | custom-call | tf_op jit(solution)/shard_map/place/pallas_call | solution.py:268
Async XLA Ops:
  2.0 1.4 %collective-permute-start = (f32[4,128]{1,0:T(4,128)S(1)}, f32[4,128]{1,0:T(4,128)S(1)}, u32[]{:S(2)}, u32[]{:S(2)}) collective-permute-start(f32[4,128]{1,0:T(4,128)S(1)} %get-tuple-element.5.own_ref), channel_id=1, source_target_pairs={{0,1},{1,0},{2,3},{3,2},{4,5},{5,4},{6,7},{7,6},{8,9},{9,8},{10,11... | collective-permute-start | bytes 6152 | tf_op jit(solution)/shard_map/ppermute | solution.py:234

commit v4 on v3

--- a/solution.py
+++ b/solution.py
@@ -12,7 +12,11 @@
 limit = 50.0
 big = 1000.0
 lanes = 128
-order = (6, 7, 11, 5, 15, 10, 14, 13, 12, 3, 1, 9, 8, 4, 0, 2)
+orders = (
+    (6, 7, 11, 5, 15, 10, 14, 1, 8, 3, 13, 9, 12, 4, 0, 2),
+    (6, 7, 11, 5, 15, 10, 14, 13, 12, 3, 1, 9, 8, 4, 0, 2),
+)
+again = (0, 1, 2, 14, 4, 5, 3, 7, 8, 9, 10, 13, 12, 11, 6, 15)
 
 
 def split_pieces(table, gap):
@@ -34,17 +38,20 @@
     shape = (dates, lanes)
     column = lax.broadcasted_iota(jnp.int32, shape, 1)
     row = lax.broadcasted_iota(jnp.int32, shape, 0)
-    tiles = [slice(at, at + lanes) for at in range(0, pixels, lanes)]
     mask_copy.wait()
-    totals = [sum(jnp.where(m_ref[:, at] > 0, 1.0, 0.0) for at in tiles)]
     value_copy.wait()
-    for b in range(bands):
-        totals.append(sum(jnp.where(m_ref[:, at] > 0, x_ref[b, :, at].astype(jnp.float32), 0.0) for at in tiles))
+    step = 4 * lanes if pixels % (4 * lanes) == 0 else lanes
+    totals = [jnp.zeros((dates, step), jnp.float32)] * (bands + 1)
+    for at in range(0, pixels, step):
+        valid = m_ref[:, at : at + step] > 0
+        totals[bands] += jnp.where(valid, 1.0, 0.0)
+        for b in range(bands):
+            totals[b] += jnp.where(valid, x_ref[b, :, at : at + step].astype(jnp.float32), 0.0)
     table = jnp.zeros(shape, jnp.float32)
     days_copy.wait()
     for d in range(dates):
         table = jnp.where((row == d) & (column == bands + 1), days_ref[d].astype(jnp.float32), table)
-    for b, total in enumerate(totals[1:] + totals[:1]):
+    for b, total in enumerate(totals):
         table = jnp.where(column == b, jnp.sum(total, 1, keepdims=True), table)
     out_ref[...] = table
 
@@ -110,11 +117,26 @@
     return items
 
 
-def middle_pair(first, second):
-    n = len(first)
-    low = [jnp.minimum(first[i], second[n - 1 - i]) for i in range(n)]
-    high = [jnp.maximum(first[i], second[n - 1 - i]) for i in range(n)]
-    return functools.reduce(jnp.maximum, low), functools.reduce(jnp.minimum, high)
+def middle_of(values, shape):
+    half = len(values) // 2
+    size = shape[0]
+    pair = (2 * size, shape[1])
+    upper = lax.broadcasted_iota(jnp.int32, pair, 0) < size
+    sign = jnp.where(upper, big, -big).astype(jnp.bfloat16)
+    items = []
+    for first, second in zip(values[:half], values[half:]):
+        value = jnp.concatenate([first, second], 0).astype(jnp.bfloat16)
+        clear = value < limit
+        items.append(jnp.where(clear, value, sign))
+        sign = jnp.where(clear, sign, -sign)
+    items = [item.astype(jnp.float32) for item in sort_list(items)]
+    sign = sign.astype(jnp.float32)
+    odd_first, odd_second = sign[:size] < 0, sign[size:] > 0
+    low = functools.reduce(jnp.maximum, [jnp.minimum(items[i][:size], items[half - 1 - i][size:]) for i in range(half)])
+    high = functools.reduce(jnp.minimum, [jnp.maximum(items[i][:size], items[half - 1 - i][size:]) for i in range(half)])
+    left = jnp.where(odd_second & ~odd_first, high, low)
+    right = jnp.where(odd_first & ~odd_second, low, high)
+    return 0.5 * (left + right)
 
 
 def blocks_of(lines):
@@ -133,30 +155,30 @@
     spread = ((pick == to) | (pick == to + gap) | (pick == to + 2 * gap)).astype(jnp.bfloat16)
     for s in range(sources):
         wide_ref[s] = in_ref[s, 0:rows, :].astype(jnp.float32)
-        table_ref[s] = jnp.dot(in_ref[s, rows : rows + dates, :], spread, preferred_element_type=jnp.float32)
+    stats = jnp.concatenate([in_ref[s, rows : rows + dates, :] for s in range(sources)], 0)
+    table_ref[...] = jnp.dot(stats, spread, preferred_element_type=jnp.float32)
     shared = None
     for start, size in blocks_of(lines):
         shape = (size, lanes)
         line = lax.broadcasted_iota(jnp.int32, shape, 0) + start
         fresh = shared is None or 8 % groups != 0 or shared[0].shape != shape
         zero = jnp.zeros(shape, jnp.float32)
-        sign = jnp.full(shape, big, jnp.float32)
         s_y, s_ty, s_zero, s_one, s_two = zero, zero, zero, zero, zero
-        items = []
+        values = []
         for s in range(sources):
             for d in range(dates):
 
                 def stat_at(b):
-                    row = table_ref[s, d : d + 1, b * lanes : (b + 1) * lanes]
+                    at = s * dates + d
+                    row = table_ref[at : at + 1, b * lanes : (b + 1) * lanes]
                     return jnp.broadcast_to(row, shape)
 
                 mean = stat_at(start // groups)
                 for b in range(start // groups + 1, (start + size - 1) // groups + 1):
                     mean = jnp.where(line >= b * groups, stat_at(b), mean)
                 value = wide_ref[s, pl.ds(start * dates + d, size, stride=dates), :]
+                values.append(value)
                 clear = value < limit
-                items.append(jnp.where(clear, value, sign))
-                sign = jnp.where(clear, sign, -sign)
                 year = stat_at(bands)
                 part = jnp.where(clear, value - mean, 0.0)
                 s_y = s_y + part
@@ -166,9 +188,7 @@
                     s_zero = s_zero + jnp.where(clear, 1.0, 0.0)
                     s_one = s_one + timed
                     s_two = s_two + timed * year
-        half = len(items) // 2
-        low, high = middle_pair(sort_list(items[:half]), sort_list(items[half:]))
-        median = 0.5 * (low + jnp.where(sign > 0, high, low))
+        median = middle_of(values, shape)
         if fresh:
             first = s_zero + ridge
             shared = (first, s_one, first * (s_two + ridge) - s_one * s_one)
@@ -179,18 +199,24 @@
             out_ref[c, lines + start : lines + start + size, :] = slope
 
 
-def place_kernel(bands, groups, in_ref, median_ref, slope_ref):
+def place_kernel(bands, groups, turns, in_ref, median_ref, slope_ref, held_ref, sems):
     lines = bands * groups
-    for s in range(in_ref.shape[0]):
-        for g in range(groups):
-            at = (s * groups + g) * lanes
-            median_ref[:, at : at + lanes] = in_ref[s, pl.ds(g, bands, stride=groups), :]
-            slope_ref[:, at : at + lanes] = in_ref[s, pl.ds(lines + g, bands, stride=groups), :]
-
-
-def call(kernel, name, out_shape, in_specs, scratch=(), flops=0, aliases={}):
+    copies = []
+    for n, to_ref in enumerate((median_ref, slope_ref)):
+        for s, part in enumerate(turns):
+            for g in range(groups):
+                at = (part * groups + g) * lanes
+                held_ref[n, :, at : at + lanes] = in_ref[s, pl.ds(n * lines + g, bands, stride=groups), :]
+        copy = pltpu.make_async_copy(held_ref.at[n], to_ref, sems.at[n])
+        copy.start()
+        copies.append(copy)
+    for copy in copies:
+        copy.wait()
+
+
+def call(kernel, name, out_shape, in_specs, scratch=(), flops=0, aliases={}, space=pltpu.VMEM):
     many = isinstance(out_shape, tuple)
-    spec = pl.BlockSpec(memory_space=pltpu.VMEM)
+    spec = pl.BlockSpec(memory_space=space)
     cost = pl.CostEstimate(flops=flops, bytes_accessed=flops, transcendentals=0) if flops else None
     return pl.pallas_call(
         kernel,
@@ -205,9 +231,12 @@
     )
 
 
-def exchange(x):
-    groups = [list(order)] if len(order) == x.shape[0] else None
-    return lax.all_to_all(x, "date", split_axis=0, concat_axis=0, tiled=True, axis_index_groups=groups)
+def exchange(x, turn, tiles):
+    parts = x.shape[0]
+    if len(orders) != tiles or len(turn) != parts:
+        return lax.all_to_all(x, "date", split_axis=0, concat_axis=0, tiled=True)
+    groups = [[order[i] * tiles + tile for i in turn] for tile, order in enumerate(orders)]
+    return lax.all_to_all(x, ("date", "pix"), split_axis=0, concat_axis=0, tiled=True, axis_index_groups=groups)
 
 
 def local(parts, tiles, reflect, cloud_free, days):
@@ -252,7 +281,8 @@
         [inside] * 3,
         aliases={2: 0},
     )(own, other, pltpu.with_memory_space_constraint(packed, inside))
-    moved = exchange(stamped)
+    turns = again if len(orders) == tiles and len(again) == parts else tuple(range(parts))
+    moved = exchange(stamped, tuple(range(parts)), tiles)
     fitted = call(
         functools.partial(fit_kernel, bands, groups, dates),
         "fit",
@@ -260,12 +290,19 @@
         [inside],
         [
             pltpu.VMEM((parts, rows, lanes), jnp.float32),
-            pltpu.VMEM((parts, dates, (bands + 1) * lanes), jnp.float32),
+            pltpu.VMEM((parts * dates, (bands + 1) * lanes), jnp.float32),
         ],
     )(moved)
-    spread = exchange(fitted)
+    spread = exchange(fitted, turns, tiles)
     shape = array((bands, pixels), jnp.float32)
-    return call(functools.partial(place_kernel, bands, groups), "place", (shape, shape), [inside])(spread)
+    return call(
+        functools.partial(place_kernel, bands, groups, turns),
+        "place",
+        (shape, shape),
+        [inside],
+        [pltpu.VMEM((2, bands, pixels), jnp.float32), pltpu.SemaphoreType.DMA((2,))],
+        space=outside,
+    )(spread)
 
 
 def solution(mesh):

time: 38.9 us -> 37.9 us (0.974)
  blocking collectives: 33.3 us -> 32.6 us
    all_to_all x2, blocking collectives: 33.3 us -> 32.6 us  [exchange(): lax.all_to_all(x, ('date', 'pix'), split_axis=0, concat_axis=0, tiled=Tru...]
where the time goes in v4:
time: 37.9 us; the launch traced here: 37.7 us
  blocking collectives  32.6 us (86%)
  Pallas kernels  3.2 us (8%)
  waiting for transfers between devices  0.66 us (2%)
  between operations  0.65 us (2%)
  starting transfers between devices  0.56 us (1%)
    all_to_all x2, blocking collectives, exchange(): lax.all_to_all(x, ('date', 'pix'), split_axis=0, concat_axis=0, tiled=Tru...  32.6 us
    pallas_call x1, Pallas kernels, local(): call(functools.partial(load_kernel, bands), 'load', (array(values.shape,...  1.28 us
    pallas_call x1, Pallas kernels, local(): call(functools.partial(place_kernel, bands, groups, turns), 'place', (sha...  0.84 us
    pallas_call x1, Pallas kernels, local(): call(functools.partial(fit_kernel, bands, groups, dates), 'fit', array((p...  0.76 us
  transfers between devices with their start and end apart: 1, of which 1 were waited for; matrix products, arithmetic and copies ran while one was open for 0% of the time, Pallas kernels for 0%

profile of v4, /device:TPU:0, one launch (start us, length us, event | category | flops | bytes accessed | tf_op | source)
XLA Modules:
  0.0 37.7 jit_solution(1225722560943130949)
XLA Ops:
  0.6 1.3 %load.1 = (bf16[6,4,8192]{2,1,0:T(4,128)(2,1)S(1)}, s32[4,8192]{1,0:T(4,128)S(1)}, f32[4,128]{1,0:T(4,128)S(1)}) custom-call(s32[4]{0:T(128)} %d_hbm.1, bf16[6,4,8192]{2,1,0:T(4,128)(2,1)} %bitcast.1, s32[4,8192]{1,0:T(4,128)} %m_hbm.1), custom_call_target="tpu_custom_call" | custom-call | tf_op jit(solution)/shard_map/load/pallas_call | solution.py:251
  1.9 0.6 %collective-permute-start = (f32[4,128]{1,0:T(4,128)S(1)}, f32[4,128]{1,0:T(4,128)S(1)}, u32[]{:S(2)}, u32[]{:S(2)}) collective-permute-start(f32[4,128]{1,0:T(4,128)S(1)} %get-tuple-element.5.own_ref), channel_id=1, source_target_pairs={{0,1},{1,0},{2,3},{3,2},{4,5},{5,4},{6,7},{7,6},{8,9},{9,8},{10,11... | collective-permute-start | bytes 6152 | tf_op jit(solution)/shard_map/ppermute | solution.py:263
  2.5 0.2 pack.1.in_ref
  2.6 0.7 %collective-permute-done.other_ref = f32[4,128]{1,0:T(4,128)S(1)} collective-permute-done((f32[4,128]{1,0:T(4,128)S(1)}, f32[4,128]{1,0:T(4,128)S(1)}, u32[]{:S(2)}, u32[]{:S(2)}) %collective-permute-start) | collective-permute-done | bytes 2080 | tf_op jit(solution)/shard_map/ppermute | solution.py:263
  3.3 0.2 stamp.1
  3.5 20.0 %all_to_all.10.in_ref = bf16[16,104,128]{2,1,0:T(8,128)(2,1)S(1)} all-to-all(bf16[16,104,128]{2,1,0:T(8,128)(2,1)S(1)} %stamp.1), channel_id=1, replica_groups={{12,14,22,10,30,20,28,2,16,6,26,18,24,8,0,4},{13,15,23,11,31,21,29,27,2..., dimensions={0} | all-to-all | bytes 851968 | tf_op jit(solution)/shard_map/all_to_all | solution.py:239
  23.5 0.8 %fit.1 = f32[16,48,128]{2,1,0:T(8,128)S(1)} custom-call(bf16[16,104,128]{2,1,0:T(8,128)(2,1)S(1)} %all_to_all.10.in_ref), custom_call_target="tpu_custom_call" | custom-call | tf_op jit(solution)/shard_map/fit/pallas_call | solution.py:286
  24.3 12.6 %all_to_all.11.in_ref = f32[16,48,128]{2,1,0:T(8,128)S(1)} all-to-all(f32[16,48,128]{2,1,0:T(8,128)S(1)} %fit.1), channel_id=1, replica_groups={{12,14,22,0,30,20,10,2,16,6,26,8,24,18,28,4},{13,15,23,1,31,21,11,27,25..., dimensions={0} | all-to-all | bytes 786432 | tf_op jit(solution)/shard_map/all_to_all | solution.py:239
  36.8 0.8 %place.1 = (f32[6,8192]{1,0:T(8,128)}, f32[6,8192]{1,0:T(8,128)}) custom-call(f32[16,48,128]{2,1,0:T(8,128)S(1)} %all_to_all.11.in_ref), custom_call_target="tpu_custom_call" | custom-call | tf_op jit(solution)/shard_map/place/pallas_call | solution.py:298
Async XLA Ops:
  1.9 1.4 %collective-permute-start = (f32[4,128]{1,0:T(4,128)S(1)}, f32[4,128]{1,0:T(4,128)S(1)}, u32[]{:S(2)}, u32[]{:S(2)}) collective-permute-start(f32[4,128]{1,0:T(4,128)S(1)} %get-tuple-element.5.own_ref), channel_id=1, source_target_pairs={{0,1},{1,0},{2,3},{3,2},{4,5},{5,4},{6,7},{7,6},{8,9},{9,8},{10,11... | collective-permute-start | bytes 6152 | tf_op jit(solution)/shard_map/ppermute | solution.py:263

commit v5 on v4

--- a/solution.py
+++ b/solution.py
@@ -13,10 +13,10 @@
 big = 1000.0
 lanes = 128
 orders = (
-    (6, 7, 11, 5, 15, 10, 14, 1, 8, 3, 13, 9, 12, 4, 0, 2),
-    (6, 7, 11, 5, 15, 10, 14, 13, 12, 3, 1, 9, 8, 4, 0, 2),
+    (0, 12, 5, 8, 9, 11, 10, 3, 15, 6, 14, 1, 2, 7, 4, 13),
+    (11, 0, 9, 1, 13, 8, 3, 6, 7, 14, 10, 4, 2, 5, 12, 15),
 )
-again = (0, 1, 2, 14, 4, 5, 3, 7, 8, 9, 10, 13, 12, 11, 6, 15)
+again = (5, 8, 7, 4, 0, 12, 10, 2, 13, 1, 9, 6, 3, 14, 15, 11)
 
 
 def split_pieces(table, gap):
@@ -65,11 +65,10 @@
             value = x_ref[b, :, c * width : (c + 1) * width].astype(jnp.float32)
             marked = jnp.where(valid, value, sentinel).astype(jnp.bfloat16)
             for g in range(groups):
-                at = (b * groups + g) * dates
-                out_ref[c, at : at + dates, :] = marked[:, g * lanes : (g + 1) * lanes]
-
-
-def stamp_kernel(bands, rows, own_ref, other_ref, in_ref, out_ref):
+                out_ref[c, b * groups + g] = marked[:, g * lanes : (g + 1) * lanes]
+
+
+def stamp_kernel(bands, lines, own_ref, other_ref, in_ref, out_ref):
     del in_ref
     own = own_ref[...]
     total = own + other_ref[...]
@@ -79,7 +78,7 @@
     stats = jnp.where(column < bands, total / jnp.maximum(count, 1.0), 0.0)
     stats = split_pieces(jnp.where(column == bands + 1, own / 365.0, stats), bands + 2)
     for c in range(out_ref.shape[0]):
-        out_ref[c, rows : rows + dates, :] = stats
+        out_ref[c, lines] = stats
 
 
 def merge_pairs(n):
@@ -154,8 +153,9 @@
     to = jnp.where(to == bands, bands + 1, to)
     spread = ((pick == to) | (pick == to + gap) | (pick == to + 2 * gap)).astype(jnp.bfloat16)
     for s in range(sources):
-        wide_ref[s] = in_ref[s, 0:rows, :].astype(jnp.float32)
-    stats = jnp.concatenate([in_ref[s, rows : rows + dates, :] for s in range(sources)], 0)
+        for line in range(lines):
+            wide_ref[s, line * dates : (line + 1) * dates, :] = in_ref[s, line].astype(jnp.float32)
+    stats = jnp.concatenate([in_ref[s, lines] for s in range(sources)], 0)
     table_ref[...] = jnp.dot(stats, spread, preferred_element_type=jnp.float32)
     shared = None
     for start, size in blocks_of(lines):
@@ -231,9 +231,12 @@
     )
 
 
+def tuned(parts, tiles):
+    return len(orders) == tiles and len(again) == parts
+
+
 def exchange(x, turn, tiles):
-    parts = x.shape[0]
-    if len(orders) != tiles or len(turn) != parts:
+    if not tuned(x.shape[0], tiles):
         return lax.all_to_all(x, "date", split_axis=0, concat_axis=0, tiled=True)
     groups = [[order[i] * tiles + tile for i in turn] for tile, order in enumerate(orders)]
     return lax.all_to_all(x, ("date", "pix"), split_axis=0, concat_axis=0, tiled=True, axis_index_groups=groups)
@@ -244,7 +247,6 @@
     groups = pixels // parts // lanes
     lines = bands * groups
     rows = lines * dates
-    height = rows + -(-dates // 8) * 8
     inside, outside = pltpu.VMEM, pltpu.HBM
     array = jax.ShapeDtypeStruct
     values = jnp.transpose(reflect, (1, 0, 2))
@@ -270,18 +272,18 @@
     packed = call(
         functools.partial(pack_kernel, bands, groups),
         "pack",
-        array((parts, height, lanes), jnp.bfloat16),
+        array((parts, lines + 1, dates, lanes), jnp.bfloat16),
         [inside, inside],
         flops=16_000_000,
     )(held, mask)
     stamped = call(
-        functools.partial(stamp_kernel, bands, rows),
+        functools.partial(stamp_kernel, bands, lines),
         "stamp",
         array(packed.shape, packed.dtype),
         [inside] * 3,
         aliases={2: 0},
     )(own, other, pltpu.with_memory_space_constraint(packed, inside))
-    turns = again if len(orders) == tiles and len(again) == parts else tuple(range(parts))
+    turns = again if tuned(parts, tiles) else tuple(range(parts))
     moved = exchange(stamped, tuple(range(parts)), tiles)
     fitted = call(
         functools.partial(fit_kernel, bands, groups, dates),

time: 37.9 us -> 36.5 us (0.963)
  blocking collectives: 32.6 us -> 31.2 us
    all_to_all x2, blocking collectives: 32.6 us -> 31.2 us  [exchange(): lax.all_to_all(x, ('date', 'pix'), split_axis=0, concat_axis=0, tiled=Tru...]
where the time goes in v5:
time: 36.5 us; the launch traced here: 36.3 us
  blocking collectives  31.2 us (85%)
  Pallas kernels  3.22 us (9%)
  waiting for transfers between devices  0.68 us (2%)
  between operations  0.65 us (2%)
  starting transfers between devices  0.56 us (2%)
    all_to_all x2, blocking collectives, exchange(): lax.all_to_all(x, ('date', 'pix'), split_axis=0, concat_axis=0, tiled=Tru...  31.2 us
    pallas_call x1, Pallas kernels, local(): call(functools.partial(load_kernel, bands), 'load', (array(values.shape,...  1.28 us
    pallas_call x1, Pallas kernels, local(): call(functools.partial(place_kernel, bands, groups, turns), 'place', (sha...  0.84 us
    pallas_call x1, Pallas kernels, local(): call(functools.partial(fit_kernel, bands, groups, dates), 'fit', array((p...  0.81 us
  transfers between devices with their start and end apart: 1, of which 1 were waited for; matrix products, arithmetic and copies ran while one was open for 0% of the time, Pallas kernels for 0%

profile of v5, /device:TPU:0, one launch (start us, length us, event | category | flops | bytes accessed | tf_op | source)
XLA Modules:
  0.0 36.3 jit_solution(16928330269307678075)
XLA Ops:
  0.6 1.3 %load.1 = (bf16[6,4,8192]{2,1,0:T(4,128)(2,1)S(1)}, s32[4,8192]{1,0:T(4,128)S(1)}, f32[4,128]{1,0:T(4,128)S(1)}) custom-call(s32[4]{0:T(128)} %d_hbm.1, bf16[6,4,8192]{2,1,0:T(4,128)(2,1)} %bitcast.1, s32[4,8192]{1,0:T(4,128)} %m_hbm.1), custom_call_target="tpu_custom_call" | custom-call | tf_op jit(solution)/shard_map/load/pallas_call | solution.py:253
  1.9 0.6 %collective-permute-start = (f32[4,128]{1,0:T(4,128)S(1)}, f32[4,128]{1,0:T(4,128)S(1)}, u32[]{:S(2)}, u32[]{:S(2)}) collective-permute-start(f32[4,128]{1,0:T(4,128)S(1)} %get-tuple-element.5.own_ref), channel_id=1, source_target_pairs={{0,1},{1,0},{2,3},{3,2},{4,5},{5,4},{6,7},{7,6},{8,9},{9,8},{10,11... | collective-permute-start | bytes 6152 | tf_op jit(solution)/shard_map/ppermute | solution.py:265
  2.5 0.1 pack.1.in_ref
  2.6 0.7 %collective-permute-done.other_ref = f32[4,128]{1,0:T(4,128)S(1)} collective-permute-done((f32[4,128]{1,0:T(4,128)S(1)}, f32[4,128]{1,0:T(4,128)S(1)}, u32[]{:S(2)}, u32[]{:S(2)}) %collective-permute-start) | collective-permute-done | bytes 2080 | tf_op jit(solution)/shard_map/ppermute | solution.py:265
  3.3 0.2 stamp.1
  3.5 18.3 %all_to_all.10.in_ref = bf16[16,25,4,128]{3,2,1,0:T(4,128)(2,1)S(1)} all-to-all(bf16[16,25,4,128]{3,2,1,0:T(4,128)(2,1)S(1)} %stamp.1), channel_id=1, replica_groups={{0,24,10,16,18,22,20,6,30,12,28,2,4,14,8,26},{23,1,19,3,27,17,7,13,15,2..., dimensions={0} | all-to-all | bytes 819200 | tf_op jit(solution)/shard_map/all_to_all | solution.py:242
  21.8 0.8 %fit.1 = f32[16,48,128]{2,1,0:T(8,128)S(1)} custom-call(bf16[16,25,4,128]{3,2,1,0:T(4,128)(2,1)S(1)} %all_to_all.10.in_ref), custom_call_target="tpu_custom_call" | custom-call | tf_op jit(solution)/shard_map/fit/pallas_call | solution.py:288
  22.6 12.9 %all_to_all.11.in_ref = f32[16,48,128]{2,1,0:T(8,128)S(1)} all-to-all(f32[16,48,128]{2,1,0:T(8,128)S(1)} %fit.1), channel_id=1, replica_groups={{22,30,6,18,0,4,28,10,14,24,12,20,16,8,26,2},{17,15,13,27,23,5,21,19,11..., dimensions={0} | all-to-all | bytes 786432 | tf_op jit(solution)/shard_map/all_to_all | solution.py:242
  35.4 0.8 %place.1 = (f32[6,8192]{1,0:T(8,128)}, f32[6,8192]{1,0:T(8,128)}) custom-call(f32[16,48,128]{2,1,0:T(8,128)S(1)} %all_to_all.11.in_ref), custom_call_target="tpu_custom_call" | custom-call | tf_op jit(solution)/shard_map/place/pallas_call | solution.py:300
Async XLA Ops:
  1.9 1.4 %collective-permute-start = (f32[4,128]{1,0:T(4,128)S(1)}, f32[4,128]{1,0:T(4,128)S(1)}, u32[]{:S(2)}, u32[]{:S(2)}) collective-permute-start(f32[4,128]{1,0:T(4,128)S(1)} %get-tuple-element.5.own_ref), channel_id=1, source_target_pairs={{0,1},{1,0},{2,3},{3,2},{4,5},{5,4},{6,7},{7,6},{8,9},{9,8},{10,11... | collective-permute-start | bytes 6152 | tf_op jit(solution)/shard_map/ppermute | solution.py:265

commit v6 on v5

--- a/solution.py
+++ b/solution.py
@@ -13,10 +13,10 @@
 big = 1000.0
 lanes = 128
 orders = (
-    (0, 12, 5, 8, 9, 11, 10, 3, 15, 6, 14, 1, 2, 7, 4, 13),
-    (11, 0, 9, 1, 13, 8, 3, 6, 7, 14, 10, 4, 2, 5, 12, 15),
+    (0, 12, 5, 8, 14, 11, 10, 2, 15, 6, 9, 1, 3, 7, 4, 13),
+    (11, 0, 15, 1, 13, 8, 3, 6, 7, 2, 10, 4, 14, 5, 12, 9),
 )
-again = (5, 8, 7, 4, 0, 12, 10, 2, 13, 1, 9, 6, 3, 14, 15, 11)
+again = (5, 8, 7, 9, 0, 12, 10, 11, 2, 13, 6, 4, 1, 14, 15, 3)
 
 
 def split_pieces(table, gap):
@@ -153,8 +153,7 @@
     to = jnp.where(to == bands, bands + 1, to)
     spread = ((pick == to) | (pick == to + gap) | (pick == to + 2 * gap)).astype(jnp.bfloat16)
     for s in range(sources):
-        for line in range(lines):
-            wide_ref[s, line * dates : (line + 1) * dates, :] = in_ref[s, line].astype(jnp.float32)
+        wide_ref[s] = in_ref[s, 0:lines].astype(jnp.float32).reshape(rows, lanes)
     stats = jnp.concatenate([in_ref[s, lines] for s in range(sources)], 0)
     table_ref[...] = jnp.dot(stats, spread, preferred_element_type=jnp.float32)
     shared = None

time: 36.5 us -> 35.7 us (0.978)
  blocking collectives: 31.2 us -> 30.3 us
    all_to_all x2, blocking collectives: 31.2 us -> 30.3 us  [exchange(): lax.all_to_all(x, ('date', 'pix'), split_axis=0, concat_axis=0, tiled=Tru...]
where the time goes in v6:
time: 35.7 us; the launch traced here: 35.4 us
  blocking collectives  30.3 us (85%)
  Pallas kernels  3.22 us (9%)
  waiting for transfers between devices  0.68 us (2%)
  between operations  0.65 us (2%)
  starting transfers between devices  0.56 us (2%)
    all_to_all x2, blocking collectives, exchange(): lax.all_to_all(x, ('date', 'pix'), split_axis=0, concat_axis=0, tiled=Tru...  30.3 us
    pallas_call x1, Pallas kernels, local(): call(functools.partial(load_kernel, bands), 'load', (array(values.shape,...  1.28 us
    pallas_call x1, Pallas kernels, local(): call(functools.partial(place_kernel, bands, groups, turns), 'place', (sha...  0.84 us
    pallas_call x1, Pallas kernels, local(): call(functools.partial(fit_kernel, bands, groups, dates), 'fit', array((p...  0.8 us
  transfers between devices with their start and end apart: 1, of which 1 were waited for; matrix products, arithmetic and copies ran while one was open for 0% of the time, Pallas kernels for 0%

profile of v6, /device:TPU:0, one launch (start us, length us, event | category | flops | bytes accessed | tf_op | source)
XLA Modules:
  0.0 35.4 jit_solution(4117559343023819807)
XLA Ops:
  0.6 1.3 %load.1 = (bf16[6,4,8192]{2,1,0:T(4,128)(2,1)S(1)}, s32[4,8192]{1,0:T(4,128)S(1)}, f32[4,128]{1,0:T(4,128)S(1)}) custom-call(s32[4]{0:T(128)} %d_hbm.1, bf16[6,4,8192]{2,1,0:T(4,128)(2,1)} %bitcast.1, s32[4,8192]{1,0:T(4,128)} %m_hbm.1), custom_call_target="tpu_custom_call" | custom-call | tf_op jit(solution)/shard_map/load/pallas_call | solution.py:252
  1.9 0.6 %collective-permute-start = (f32[4,128]{1,0:T(4,128)S(1)}, f32[4,128]{1,0:T(4,128)S(1)}, u32[]{:S(2)}, u32[]{:S(2)}) collective-permute-start(f32[4,128]{1,0:T(4,128)S(1)} %get-tuple-element.5.own_ref), channel_id=1, source_target_pairs={{0,1},{1,0},{2,3},{3,2},{4,5},{5,4},{6,7},{7,6},{8,9},{9,8},{10,11... | collective-permute-start | bytes 6152 | tf_op jit(solution)/shard_map/ppermute | solution.py:264
  2.5 0.1 pack.1.in_ref
  2.6 0.7 %collective-permute-done.other_ref = f32[4,128]{1,0:T(4,128)S(1)} collective-permute-done((f32[4,128]{1,0:T(4,128)S(1)}, f32[4,128]{1,0:T(4,128)S(1)}, u32[]{:S(2)}, u32[]{:S(2)}) %collective-permute-start) | collective-permute-done | bytes 2080 | tf_op jit(solution)/shard_map/ppermute | solution.py:264
  3.3 0.2 stamp.1
  3.5 18.2 %all_to_all.10.in_ref = bf16[16,25,4,128]{3,2,1,0:T(4,128)(2,1)S(1)} all-to-all(bf16[16,25,4,128]{3,2,1,0:T(4,128)(2,1)S(1)} %stamp.1), channel_id=1, replica_groups={{0,24,10,16,28,22,20,4,30,12,18,2,6,14,8,26},{23,1,31,3,27,17,7,13,15,5..., dimensions={0} | all-to-all | bytes 819200 | tf_op jit(solution)/shard_map/all_to_all | solution.py:241
  21.7 0.8 %fit.1 = f32[16,48,128]{2,1,0:T(8,128)S(1)} custom-call(bf16[16,25,4,128]{3,2,1,0:T(4,128)(2,1)S(1)} %all_to_all.10.in_ref), custom_call_target="tpu_custom_call" | custom-call | tf_op jit(solution)/shard_map/fit/pallas_call | solution.py:287
  22.5 12.1 %all_to_all.11.in_ref = f32[16,48,128]{2,1,0:T(8,128)S(1)} all-to-all(f32[16,48,128]{2,1,0:T(8,128)S(1)} %fit.1), channel_id=1, replica_groups={{22,30,4,12,0,6,18,2,10,14,20,28,24,8,26,16},{17,15,13,5,23,29,21,9,31,..., dimensions={0} | all-to-all | bytes 786432 | tf_op jit(solution)/shard_map/all_to_all | solution.py:241
  34.6 0.8 %place.1 = (f32[6,8192]{1,0:T(8,128)}, f32[6,8192]{1,0:T(8,128)}) custom-call(f32[16,48,128]{2,1,0:T(8,128)S(1)} %all_to_all.11.in_ref), custom_call_target="tpu_custom_call" | custom-call | tf_op jit(solution)/shard_map/place/pallas_call | solution.py:299
Async XLA Ops:
  1.9 1.4 %collective-permute-start = (f32[4,128]{1,0:T(4,128)S(1)}, f32[4,128]{1,0:T(4,128)S(1)}, u32[]{:S(2)}, u32[]{:S(2)}) collective-permute-start(f32[4,128]{1,0:T(4,128)S(1)} %get-tuple-element.5.own_ref), channel_id=1, source_target_pairs={{0,1},{1,0},{2,3},{3,2},{4,5},{5,4},{6,7},{7,6},{8,9},{9,8},{10,11... | collective-permute-start | bytes 6152 | tf_op jit(solution)/shard_map/ppermute | solution.py:264

commit v7 on v6

--- a/solution.py
+++ b/solution.py
@@ -128,11 +128,15 @@
         clear = value < limit
         items.append(jnp.where(clear, value, sign))
         sign = jnp.where(clear, sign, -sign)
-    items = [item.astype(jnp.float32) for item in sort_list(items)]
+    items = sort_list(items)
     sign = sign.astype(jnp.float32)
     odd_first, odd_second = sign[:size] < 0, sign[size:] > 0
-    low = functools.reduce(jnp.maximum, [jnp.minimum(items[i][:size], items[half - 1 - i][size:]) for i in range(half)])
-    high = functools.reduce(jnp.minimum, [jnp.maximum(items[i][:size], items[half - 1 - i][size:]) for i in range(half)])
+    near = items[: (half + 1) // 2]
+    far = [jnp.concatenate([item[size:], item[:size]], 0) for item in items[half // 2 :][::-1]]
+    low = functools.reduce(jnp.maximum, [jnp.minimum(x, y) for x, y in zip(near, far)]).astype(jnp.float32)
+    high = functools.reduce(jnp.minimum, [jnp.maximum(x, y) for x, y in zip(near, far)]).astype(jnp.float32)
+    low = jnp.maximum(low[:size], low[size:])
+    high = jnp.minimum(high[:size], high[size:])
     left = jnp.where(odd_second & ~odd_first, high, low)
     right = jnp.where(odd_first & ~odd_second, low, high)
     return 0.5 * (left + right)

time: 35.7 us -> 35.6 us (level)
  no operation moved by 1% of the time
where the time goes in v7:
time: 35.6 us; the launch traced here: 35.4 us
  blocking collectives  30.3 us (85%)
  Pallas kernels  3.15 us (9%)
  waiting for transfers between devices  0.68 us (2%)
  between operations  0.65 us (2%)
  starting transfers between devices  0.56 us (2%)
    all_to_all x2, blocking collectives, exchange(): lax.all_to_all(x, ('date', 'pix'), split_axis=0, concat_axis=0, tiled=Tru...  30.3 us
    pallas_call x1, Pallas kernels, local(): call(functools.partial(load_kernel, bands), 'load', (array(values.shape,...  1.28 us
    pallas_call x1, Pallas kernels, local(): call(functools.partial(place_kernel, bands, groups, turns), 'place', (sha...  0.84 us
    pallas_call x1, Pallas kernels, local(): call(functools.partial(fit_kernel, bands, groups, dates), 'fit', array((p...  0.73 us
  transfers between devices with their start and end apart: 1, of which 1 were waited for; matrix products, arithmetic and copies ran while one was open for 0% of the time, Pallas kernels for 0%

profile of v7, /device:TPU:0, one launch (start us, length us, event | category | flops | bytes accessed | tf_op | source)
XLA Modules:
  0.0 35.4 jit_solution(1852439316345979669)
XLA Ops:
  0.6 1.3 %load.1 = (bf16[6,4,8192]{2,1,0:T(4,128)(2,1)S(1)}, s32[4,8192]{1,0:T(4,128)S(1)}, f32[4,128]{1,0:T(4,128)S(1)}) custom-call(s32[4]{0:T(128)} %d_hbm.1, bf16[6,4,8192]{2,1,0:T(4,128)(2,1)} %bitcast.1, s32[4,8192]{1,0:T(4,128)} %m_hbm.1), custom_call_target="tpu_custom_call" | custom-call | tf_op jit(solution)/shard_map/load/pallas_call | solution.py:256
  1.9 0.6 %collective-permute-start = (f32[4,128]{1,0:T(4,128)S(1)}, f32[4,128]{1,0:T(4,128)S(1)}, u32[]{:S(2)}, u32[]{:S(2)}) collective-permute-start(f32[4,128]{1,0:T(4,128)S(1)} %get-tuple-element.5.own_ref), channel_id=1, source_target_pairs={{0,1},{1,0},{2,3},{3,2},{4,5},{5,4},{6,7},{7,6},{8,9},{9,8},{10,11... | collective-permute-start | bytes 6152 | tf_op jit(solution)/shard_map/ppermute | solution.py:268
  2.5 0.1 pack.1.in_ref
  2.6 0.7 %collective-permute-done.other_ref = f32[4,128]{1,0:T(4,128)S(1)} collective-permute-done((f32[4,128]{1,0:T(4,128)S(1)}, f32[4,128]{1,0:T(4,128)S(1)}, u32[]{:S(2)}, u32[]{:S(2)}) %collective-permute-start) | collective-permute-done | bytes 2080 | tf_op jit(solution)/shard_map/ppermute | solution.py:268
  3.3 0.2 stamp.1
  3.5 18.2 %all_to_all.10.in_ref = bf16[16,25,4,128]{3,2,1,0:T(4,128)(2,1)S(1)} all-to-all(bf16[16,25,4,128]{3,2,1,0:T(4,128)(2,1)S(1)} %stamp.1), channel_id=1, replica_groups={{0,24,10,16,28,22,20,4,30,12,18,2,6,14,8,26},{23,1,31,3,27,17,7,13,15,5..., dimensions={0} | all-to-all | bytes 819200 | tf_op jit(solution)/shard_map/all_to_all | solution.py:245
  21.7 0.7 %fit.1 = f32[16,48,128]{2,1,0:T(8,128)S(1)} custom-call(bf16[16,25,4,128]{3,2,1,0:T(4,128)(2,1)S(1)} %all_to_all.10.in_ref), custom_call_target="tpu_custom_call" | custom-call | tf_op jit(solution)/shard_map/fit/pallas_call | solution.py:291
  22.4 12.1 %all_to_all.11.in_ref = f32[16,48,128]{2,1,0:T(8,128)S(1)} all-to-all(f32[16,48,128]{2,1,0:T(8,128)S(1)} %fit.1), channel_id=1, replica_groups={{22,30,4,12,0,6,18,2,10,14,20,28,24,8,26,16},{17,15,13,5,23,29,21,9,31,..., dimensions={0} | all-to-all | bytes 786432 | tf_op jit(solution)/shard_map/all_to_all | solution.py:245
  34.5 0.8 %place.1 = (f32[6,8192]{1,0:T(8,128)}, f32[6,8192]{1,0:T(8,128)}) custom-call(f32[16,48,128]{2,1,0:T(8,128)S(1)} %all_to_all.11.in_ref), custom_call_target="tpu_custom_call" | custom-call | tf_op jit(solution)/shard_map/place/pallas_call | solution.py:303
Async XLA Ops:
  1.9 1.4 %collective-permute-start = (f32[4,128]{1,0:T(4,128)S(1)}, f32[4,128]{1,0:T(4,128)S(1)}, u32[]{:S(2)}, u32[]{:S(2)}) collective-permute-start(f32[4,128]{1,0:T(4,128)S(1)} %get-tuple-element.5.own_ref), channel_id=1, source_target_pairs={{0,1},{1,0},{2,3},{3,2},{4,5},{5,4},{6,7},{7,6},{8,9},{9,8},{10,11... | collective-permute-start | bytes 6152 | tf_op jit(solution)/shard_map/ppermute | solution.py:268

commit v8 on v7

--- a/solution.py
+++ b/solution.py
@@ -202,17 +202,22 @@
             out_ref[c, lines + start : lines + start + size, :] = slope
 
 
-def place_kernel(bands, groups, turns, in_ref, median_ref, slope_ref, held_ref, sems):
+def place_kernel(bands, groups, turns, pieces, in_ref, median_ref, slope_ref, held_ref, sems):
     lines = bands * groups
+    source = {part: s for s, part in enumerate(turns)}
+    share = len(turns) // pieces
     copies = []
-    for n, to_ref in enumerate((median_ref, slope_ref)):
-        for s, part in enumerate(turns):
-            for g in range(groups):
-                at = (part * groups + g) * lanes
-                held_ref[n, :, at : at + lanes] = in_ref[s, pl.ds(n * lines + g, bands, stride=groups), :]
-        copy = pltpu.make_async_copy(held_ref.at[n], to_ref, sems.at[n])
-        copy.start()
-        copies.append(copy)
+    for piece in range(pieces):
+        for n, to_ref in enumerate((median_ref, slope_ref)):
+            for part in range(piece * share, (piece + 1) * share):
+                for g in range(groups):
+                    at = (part * groups + g) * lanes
+                    line = in_ref[source[part], pl.ds(n * lines + g, bands, stride=groups), :]
+                    held_ref[n, :, at : at + lanes] = line
+            where = pl.ds(piece * share * groups * lanes, share * groups * lanes)
+            copy = pltpu.make_async_copy(held_ref.at[n, :, where], to_ref.at[:, where], sems.at[n, piece])
+            copy.start()
+            copies.append(copy)
     for copy in copies:
         copy.wait()
 
@@ -301,11 +306,11 @@
     spread = exchange(fitted, turns, tiles)
     shape = array((bands, pixels), jnp.float32)
     return call(
-        functools.partial(place_kernel, bands, groups, turns),
+        functools.partial(place_kernel, bands, groups, turns, 2),
         "place",
         (shape, shape),
         [inside],
-        [pltpu.VMEM((2, bands, pixels), jnp.float32), pltpu.SemaphoreType.DMA((2,))],
+        [pltpu.VMEM((2, bands, pixels), jnp.float32), pltpu.SemaphoreType.DMA((2, 2))],
         space=outside,
     )(spread)
 

time: 35.6 us -> 35.6 us (level)
  no operation moved by 1% of the time
where the time goes in v8:
time: 35.6 us; the launch traced here: 35.4 us
  blocking collectives  30.3 us (85%)
  Pallas kernels  3.15 us (9%)
  waiting for transfers between devices  0.68 us (2%)
  between operations  0.65 us (2%)
  starting transfers between devices  0.56 us (2%)
    all_to_all x2, blocking collectives, exchange(): lax.all_to_all(x, ('date', 'pix'), split_axis=0, concat_axis=0, tiled=Tru...  30.3 us
    pallas_call x1, Pallas kernels, local(): call(functools.partial(load_kernel, bands), 'load', (array(values.shape,...  1.28 us
    pallas_call x1, Pallas kernels, local(): call(functools.partial(place_kernel, bands, groups, turns, 2), 'place', (...  0.83 us
    pallas_call x1, Pallas kernels, local(): call(functools.partial(fit_kernel, bands, groups, dates), 'fit', array((p...  0.73 us
  transfers between devices with their start and end apart: 1, of which 1 were waited for; matrix products, arithmetic and copies ran while one was open for 0% of the time, Pallas kernels for 0%

profile of v8, /device:TPU:0, one launch (start us, length us, event | category | flops | bytes accessed | tf_op | source)
XLA Modules:
  0.0 35.4 jit_solution(9058292407374175031)
XLA Ops:
  0.6 1.3 %load.1 = (bf16[6,4,8192]{2,1,0:T(4,128)(2,1)S(1)}, s32[4,8192]{1,0:T(4,128)S(1)}, f32[4,128]{1,0:T(4,128)S(1)}) custom-call(s32[4]{0:T(128)} %d_hbm.1, bf16[6,4,8192]{2,1,0:T(4,128)(2,1)} %bitcast.1, s32[4,8192]{1,0:T(4,128)} %m_hbm.1), custom_call_target="tpu_custom_call" | custom-call | tf_op jit(solution)/shard_map/load/pallas_call | solution.py:261
  1.9 0.6 %collective-permute-start = (f32[4,128]{1,0:T(4,128)S(1)}, f32[4,128]{1,0:T(4,128)S(1)}, u32[]{:S(2)}, u32[]{:S(2)}) collective-permute-start(f32[4,128]{1,0:T(4,128)S(1)} %get-tuple-element.5.own_ref), channel_id=1, source_target_pairs={{0,1},{1,0},{2,3},{3,2},{4,5},{5,4},{6,7},{7,6},{8,9},{9,8},{10,11... | collective-permute-start | bytes 6152 | tf_op jit(solution)/shard_map/ppermute | solution.py:273
  2.5 0.1 pack.1.in_ref
  2.6 0.7 %collective-permute-done.other_ref = f32[4,128]{1,0:T(4,128)S(1)} collective-permute-done((f32[4,128]{1,0:T(4,128)S(1)}, f32[4,128]{1,0:T(4,128)S(1)}, u32[]{:S(2)}, u32[]{:S(2)}) %collective-permute-start) | collective-permute-done | bytes 2080 | tf_op jit(solution)/shard_map/ppermute | solution.py:273
  3.3 0.2 stamp.1
  3.5 18.2 %all_to_all.10.in_ref = bf16[16,25,4,128]{3,2,1,0:T(4,128)(2,1)S(1)} all-to-all(bf16[16,25,4,128]{3,2,1,0:T(4,128)(2,1)S(1)} %stamp.1), channel_id=1, replica_groups={{0,24,10,16,28,22,20,4,30,12,18,2,6,14,8,26},{23,1,31,3,27,17,7,13,15,5..., dimensions={0} | all-to-all | bytes 819200 | tf_op jit(solution)/shard_map/all_to_all | solution.py:250
  21.7 0.7 %fit.1 = f32[16,48,128]{2,1,0:T(8,128)S(1)} custom-call(bf16[16,25,4,128]{3,2,1,0:T(4,128)(2,1)S(1)} %all_to_all.10.in_ref), custom_call_target="tpu_custom_call" | custom-call | tf_op jit(solution)/shard_map/fit/pallas_call | solution.py:296
  22.4 12.1 %all_to_all.11.in_ref = f32[16,48,128]{2,1,0:T(8,128)S(1)} all-to-all(f32[16,48,128]{2,1,0:T(8,128)S(1)} %fit.1), channel_id=1, replica_groups={{22,30,4,12,0,6,18,2,10,14,20,28,24,8,26,16},{17,15,13,5,23,29,21,9,31,..., dimensions={0} | all-to-all | bytes 786432 | tf_op jit(solution)/shard_map/all_to_all | solution.py:250
  34.5 0.8 %place.1 = (f32[6,8192]{1,0:T(8,128)}, f32[6,8192]{1,0:T(8,128)}) custom-call(f32[16,48,128]{2,1,0:T(8,128)S(1)} %all_to_all.11.in_ref), custom_call_target="tpu_custom_call" | custom-call | tf_op jit(solution)/shard_map/place/pallas_call | solution.py:308
Async XLA Ops:
  1.9 1.4 %collective-permute-start = (f32[4,128]{1,0:T(4,128)S(1)}, f32[4,128]{1,0:T(4,128)S(1)}, u32[]{:S(2)}, u32[]{:S(2)}) collective-permute-start(f32[4,128]{1,0:T(4,128)S(1)} %get-tuple-element.5.own_ref), channel_id=1, source_target_pairs={{0,1},{1,0},{2,3},{3,2},{4,5},{5,4},{6,7},{7,6},{8,9},{9,8},{10,11... | collective-permute-start | bytes 6152 | tf_op jit(solution)/shard_map/ppermute | solution.py:273
